TPU v7x, 16 devices: a whole 2x2x2 slice. The times are simulated.
16 devices in a mesh: data: 16 (over z, y, x, core).
Axes of the slice: x: 2, y: 2, z: 2, core: 2. Of those that a mesh axis runs over, the one named last changes fastest.
Arguments:
- x_now: bfloat16 [64, 197, 192], P('data')
- x_next: bfloat16 [64, 197, 192], P('data')
- labels: int32 [64], P('data')
- w_up: float32 [32, 192, 768], replicated
- w_down: float32 [32, 768, 192], replicated
- w_head: float32 [192, 1000], replicated
- mom_up: float32 [32, 192, 768], P(None, None, 'data')
- mom_down: float32 [32, 768, 192], P(None, 'data')
- mom_head: float32 [192, 1000], P('data')
- learn_rate: float32 [], replicated
- mom_decay: float32 [], replicated
Outputs:
- output 1: float32 [64, 1000], P('data')
- output 2: float32 [32, 192, 768], replicated
- output 3: float32 [32, 768, 192], replicated
- output 4: float32 [192, 1000], replicated
- output 5: float32 [32, 192, 768], P(None, None, 'data')
- output 6: float32 [32, 768, 192], P(None, 'data')
- output 7: float32 [192, 1000], P('data')
All inputs are finite; a program needn't handle non-finite values.
Results may differ from a plain program's by a relative error of at most 0.0158812.
Values are sent between devices in bfloat16 or wider.
A program may use at most 1 GiB of HBM per device.

v0:
```python
import jax
import jax.numpy as jnp
from jax import lax
from jax.sharding import PartitionSpec as P

LN_EPS = 1e-6
CONTRACT_ROWS = (((0,), (0,)), ((), ()))
CONTRACT_LAST = (((1,), (1,)), ((), ()))


def norm_rows(values):
    mean_v = jnp.mean(values, axis=-1, keepdims=True)
    centered = values - mean_v
    var_v = jnp.mean(centered * centered, axis=-1, keepdims=True)
    return centered * lax.rsqrt(var_v + LN_EPS)


def gelu_tanh(values):
    return jax.nn.gelu(values, approximate=True)


def block_forward(x_rows, up_w, down_w):
    x_wide = x_rows.astype(jnp.float32)
    u_rows = norm_rows(x_wide).astype(jnp.bfloat16)
    pre_act = jnp.dot(u_rows, up_w, preferred_element_type=jnp.float32).astype(jnp.bfloat16)
    gelu_out = gelu_tanh(pre_act.astype(jnp.float32)).astype(jnp.bfloat16)
    block_out = jnp.dot(gelu_out, down_w, preferred_element_type=jnp.float32).astype(jnp.bfloat16)
    new_rows = (x_wide + block_out.astype(jnp.float32)).astype(jnp.bfloat16)
    return new_rows, (x_rows, u_rows, pre_act, gelu_out)


def forward_rows(x_in, up_b, down_b):
    n_img, n_tok, width = x_in.shape
    rows = x_in.reshape(n_img * n_tok, width)
    saved_acts = []
    for layer in range(up_b.shape[0]):
        rows, layer_acts = block_forward(rows, up_b[layer], down_b[layer])
        saved_acts.append(layer_acts)
    return rows, saved_acts


def head_forward(rows, head_b, n_img):
    pooled = jnp.mean(rows.reshape(n_img, -1, rows.shape[-1]), axis=1, dtype=jnp.float32)
    normed = norm_rows(pooled).astype(jnp.bfloat16)
    return jnp.dot(normed, head_b, preferred_element_type=jnp.float32), pooled, normed


def backward_layers(saved_acts, up_b, down_b, grad_rows):
    up_grads = []
    down_grads = []
    for layer in reversed(range(len(saved_acts))):
        x_rows, u_rows, pre_act, gelu_out = saved_acts[layer]
        down_grads.append(lax.dot_general(gelu_out, grad_rows, CONTRACT_ROWS, preferred_element_type=jnp.float32).astype(jnp.bfloat16))
        grad_gelu = lax.dot_general(grad_rows, down_b[layer], CONTRACT_LAST, preferred_element_type=jnp.float32).astype(jnp.bfloat16)
        _, gelu_pull = jax.vjp(gelu_tanh, pre_act.astype(jnp.float32))
        grad_pre = gelu_pull(grad_gelu.astype(jnp.float32))[0].astype(jnp.bfloat16)
        up_grads.append(lax.dot_general(u_rows, grad_pre, CONTRACT_ROWS, preferred_element_type=jnp.float32).astype(jnp.bfloat16))
        if layer > 0:
            grad_u = lax.dot_general(grad_pre, up_b[layer], CONTRACT_LAST, preferred_element_type=jnp.float32).astype(jnp.bfloat16)
            _, norm_pull = jax.vjp(norm_rows, x_rows.astype(jnp.float32))
            grad_norm = norm_pull(grad_u.astype(jnp.float32))[0]
            grad_rows = (grad_rows.astype(jnp.float32) + grad_norm).astype(jnp.bfloat16)
    return jnp.stack(up_grads[::-1]), jnp.stack(down_grads[::-1])


def solution(mesh):
    n_dev = mesh.shape["data"]

    def local_step(x_now, x_next, labels, w_up, w_down, w_head, mom_up, mom_down, mom_head, learn_rate, mom_decay):
        n_img, n_tok, width = x_now.shape
        batch_total = n_img * n_dev
        up_b = w_up.astype(jnp.bfloat16)
        down_b = w_down.astype(jnp.bfloat16)
        head_b = w_head.astype(jnp.bfloat16)
        rows, saved_acts = forward_rows(x_now, up_b, down_b)
        logits, pooled, normed = head_forward(rows, head_b, n_img)
        soft_probs = jax.nn.softmax(logits, axis=-1)
        targets = jax.nn.one_hot(labels, logits.shape[-1], dtype=jnp.float32)
        grad_logits = ((soft_probs - targets) / batch_total).astype(jnp.bfloat16)
        head_grad = lax.dot_general(normed, grad_logits, CONTRACT_ROWS, preferred_element_type=jnp.float32).astype(jnp.bfloat16)
        grad_normed = lax.dot_general(grad_logits, head_b, CONTRACT_LAST, preferred_element_type=jnp.float32).astype(jnp.bfloat16)
        _, norm_pull = jax.vjp(norm_rows, pooled)
        grad_pooled = norm_pull(grad_normed.astype(jnp.float32))[0]
        grad_rows = jnp.broadcast_to((grad_pooled / n_tok)[:, None, :], (n_img, n_tok, width))
        grad_rows = grad_rows.astype(jnp.bfloat16).reshape(n_img * n_tok, width)
        up_grad, down_grad = backward_layers(saved_acts, up_b, down_b, grad_rows)
        up_sum = lax.psum_scatter(up_grad, "data", scatter_dimension=2, tiled=True)
        down_sum = lax.psum_scatter(down_grad, "data", scatter_dimension=1, tiled=True)
        head_sum = lax.psum_scatter(head_grad, "data", scatter_dimension=0, tiled=True)
        shard_index = lax.axis_index("data")
        new_mom_up = mom_decay * mom_up + up_sum.astype(jnp.float32)
        new_mom_down = mom_decay * mom_down + down_sum.astype(jnp.float32)
        new_mom_head = mom_decay * mom_head + head_sum.astype(jnp.float32)
        up_width = mom_up.shape[2]
        down_width = mom_down.shape[1]
        head_width = mom_head.shape[0]
        up_part = lax.dynamic_slice_in_dim(w_up, shard_index * up_width, up_width, axis=2) - learn_rate * new_mom_up
        down_part = lax.dynamic_slice_in_dim(w_down, shard_index * down_width, down_width, axis=1) - learn_rate * new_mom_down
        head_part = lax.dynamic_slice_in_dim(w_head, shard_index * head_width, head_width, axis=0) - learn_rate * new_mom_head
        new_w_up = lax.all_gather(up_part, "data", axis=2, tiled=True)
        new_w_down = lax.all_gather(down_part, "data", axis=1, tiled=True)
        new_w_head = lax.all_gather(head_part, "data", axis=0, tiled=True)
        next_rows, _ = forward_rows(x_next, new_w_up.astype(jnp.bfloat16), new_w_down.astype(jnp.bfloat16))
        logits_next = head_forward(next_rows, new_w_head.astype(jnp.bfloat16), n_img)[0]
        return (logits_next, new_w_up, new_w_down, new_w_head, new_mom_up, new_mom_down, new_mom_head)

    spec_up = P(None, None, "data")
    spec_down = P(None, "data", None)
    spec_head = P("data", None)
    return jax.shard_map(
        local_step,
        mesh=mesh,
        in_specs=(P("data"), P("data"), P("data"), P(), P(), P(), spec_up, spec_down, spec_head, P(), P()),
        out_specs=(P("data"), P(), P(), P(), spec_up, spec_down, spec_head),
        check_vma=False,
    )
```

profile of v0, /device:TPU:0, one launch (start us, length us, event | category | flops | bytes accessed | tf_op | source)
XLA Modules:
  0.0 920.0 jit_solution(2824460486571238706)
XLA Ops:
  13.2 9.8 %convert_element_type.2551 = bf16[32,192,768]{2,1,0:T(8,128)(2,1)} convert(f32[32,192,768]{2,1,0:T(8,128)} %param.14) | non-fusion elementwise | flops 4718592 | bytes 28311552 | tf_op jit(solution)/shard_map/convert_element_type | solution.py:72
  23.6 9.8 %convert_element_type.2555 = bf16[32,768,192]{1,2,0:T(8,128)(2,1)} convert(f32[32,768,192]{1,2,0:T(8,128)} %param.15) | non-fusion elementwise | flops 4718592 | bytes 28311552 | tf_op jit(solution)/shard_map/convert_element_type | solution.py:73
  67.4 2.6 fusion.1569
  104.8 2.5 fusion.1576
  137.8 2.5 fusion.1583
  168.2 2.7 fusion.1590
  198.5 3.5 fusion.35
  204.6 3.5 fusion.38
  324.5 4.8 fusion.1035
  329.3 2.6 fusion.1037
  331.9 2.6 fusion.1039
  371.5 17.3 %copy.59 = bf16[32,192,768]{1,0,2:T(8,128)(2,1)} copy(bf16[32,192,768]{2,1,0:T(8,128)(2,1)} %fusion.1097) | data formatting | bytes 18874368 | tf_op jit(solution)/shard_map/stack | solution.py:63
  390.1 2.8 fusion.1099
  451.1 17.3 %copy.63 = bf16[32,768,192]{2,0,1:T(8,128)(2,1)} copy(bf16[32,768,192]{1,2,0:T(8,128)(2,1)} %fusion.1161) | data formatting | bytes 18874368 | tf_op jit(solution)/shard_map/stack | solution.py:63
  468.7 3.7 constant_dynamic-slice_fusion.1
  472.4 2.6 copy.70
  476.3 6.0 reduce-scatter.5.cloned.1.call-done
  482.3 4.9 multiply_subtract_fusion.1
  487.2 3.7 constant_dynamic-slice_fusion
  490.9 2.6 copy.71
  493.5 84.5 %reduce-scatter.7.cloned.1.call-done = bf16[32,48,192]{2,0,1:T(8,128)(2,1)} async-done(((bf16[32,768,192]{2,0,1:T(8,128)(2,1)}), bf16[32,48,192]{2,0,1:T(8,128)(2,1)}) %reduce-scatter.7.cloned.1.call-update) | async-done | bytes 589840 | tf_op jit(solution)/shard_map/reduce_scatter | solution.py:88
  577.9 4.3 multiply_subtract_fusion
  582.7 36.5 %fusion = bf16[16,1000]{1,0:T(8,128)(2,1)S(1)} fusion(bf16[192,1000]{1,0:T(8,128)(2,1)S(1)} %convolution_convert_fusion.96), kind=kCustom, calls=%all-reduce-scatter | all-reduce-scatter fusion | flops 256001 | bytes 416000
  624.9 6.0 collective-permute-start.3
  633.1 2.6 reshape.1263
  635.7 7.2 concatenate
  644.4 17.3 %all-gather = f32[16,12,1000]{2,1,0:T(8,128)} all-gather(f32[1,12,1000]{2,1,0:T(8,128)S(1)} %get-tuple-element.41), channel_id=1, replica_groups=mesh['data'=16] {'data'}, dimensions={0}, use_global_device_ids=true | all-gather | bytes 816000 | tf_op jit(solution)/shard_map/all_gather | solution.py:102
  668.1 23.5 %all-gather.4.cloned.1.call-done = f32[32,192,768]{1,0,2:T(8,128)} async-done(((f32[32,192,48]{1,0,2:T(8,128)}), f32[32,192,768]{1,0,2:T(8,128)}) %all-gather.4.cloned.1.call-update) | async-done | bytes 18874384 | tf_op jit(solution)/shard_map/all_gather | solution.py:100
  691.5 22.8 %copy.60 = f32[32,192,768]{2,1,0:T(8,128)} copy(f32[32,192,768]{1,0,2:T(8,128)} %all-gather.4.cloned.1.call-done) | data formatting | bytes 37748736 | tf_op jit(solution)/shard_map/all_gather | solution.py:100
  714.3 9.9 %convert_element_type.3069 = bf16[32,192,768]{2,1,0:T(8,128)(2,1)} convert(f32[32,192,768]{2,1,0:T(8,128)} %copy.60) | non-fusion elementwise | flops 4718592 | bytes 28311552 | tf_op jit(solution)/shard_map/convert_element_type | solution.py:103
  724.2 73.3 %all-gather.6.cloned.1.call-done = f32[32,768,192]{2,0,1:T(8,128)} async-done(((f32[32,48,192]{2,0,1:T(8,128)}), f32[32,768,192]{2,0,1:T(8,128)}) %all-gather.6.cloned.1.call-update) | async-done | bytes 18874384 | tf_op jit(solution)/shard_map/all_gather | solution.py:101
  797.5 22.8 %copy.64 = f32[32,768,192]{1,2,0:T(8,128)} copy(f32[32,768,192]{2,0,1:T(8,128)} %all-gather.6.cloned.1.call-done) | data formatting | bytes 37748736 | tf_op jit(solution)/shard_map/all_gather | solution.py:101
  820.4 10.3 %convert_element_type.3106 = bf16[32,768,192]{1,2,0:T(8,128)(2,1)} convert(f32[32,768,192]{1,2,0:T(8,128)} %copy.64) | non-fusion elementwise | flops 4718592 | bytes 28311552 | tf_op jit(solution)/shard_map/convert_element_type | solution.py:103
  840.6 2.4 fusion.1599
  843.1 2.4 fusion.1600
  845.6 2.4 fusion.1601
  848.1 2.4 fusion.1602
  850.6 2.4 fusion.1603
  853.1 2.5 fusion.1604
  863.2 2.4 fusion.1608
  865.7 2.4 fusion.1609
  868.2 2.4 fusion.1610
  870.6 2.4 fusion.1611
  873.1 2.4 fusion.1612
  875.6 2.6 fusion.1613
  888.3 2.4 fusion.1618
  893.3 2.4 fusion.1620
  898.3 2.6 fusion.1622
  (1636 shorter events, 431.9 us)
Async XLA Ops:
  7.2 475.1 %reduce-scatter.5.cloned.1.call-start = ((), (), s32[]{:S(2)}) async-start(), calls=%async_computation.2 | async-start | bytes 13369344 | tf_op jit(solution)/shard_map/reduce_scatter | solution.py:87
  38.0 5.3 copy-start
  43.3 5.2 copy-start.2
  48.5 5.3 copy-start.4
  53.8 5.3 copy-start.6
  59.1 5.3 copy-start.9
  64.4 5.6 copy-start.12
  70.1 5.3 copy-start.15
  75.4 5.3 copy-start.18
  80.7 5.3 copy-start.21
  86.0 5.3 copy-start.24
  91.3 5.2 copy-start.27
  96.5 5.3 copy-start.30
  101.8 5.5 copy-start.33
  107.3 5.3 copy-start.36
  117.3 147.5 %copy-start.42 = (f32[788,192]{0,1:T(8,128)}, f32[788,192]{0,1:T(8,128)S(1)}, u32[]{:S(2)}) copy-start(f32[788,192]{0,1:T(8,128)S(1)} %get-tuple-element.74) | copy-start | bytes 1815556
  122.5 138.5 %copy-start.44 = (f32[788,192]{0,1:T(8,128)}, f32[788,192]{0,1:T(8,128)S(1)}, u32[]{:S(2)}) copy-start(f32[788,192]{0,1:T(8,128)S(1)} %get-tuple-element.76) | copy-start | bytes 1815556
  127.8 129.2 %copy-start.46 = (f32[788,192]{0,1:T(8,128)}, f32[788,192]{0,1:T(8,128)S(1)}, u32[]{:S(2)}) copy-start(f32[788,192]{0,1:T(8,128)S(1)} %get-tuple-element.78) | copy-start | bytes 1815556
  148.6 5.3 copy-start.60
  154.0 78.2 %copy-start.340 = (f32[788]{0:T(1024)}, f32[788]{0:T(1024)S(1)}, u32[]{:S(2)}) copy-start(f32[788]{0:T(1024)S(1)} %broadcast_multiply_fusion.38) | copy-start | bytes 9460
  158.1 70.3 %copy-start.342 = (f32[788]{0:T(1024)}, f32[788]{0:T(1024)S(1)}, u32[]{:S(2)}) copy-start(f32[788]{0:T(1024)S(1)} %broadcast_multiply_fusion.37) | copy-start | bytes 9460
  162.3 62.3 %copy-start.344 = (f32[788]{0:T(1024)}, f32[788]{0:T(1024)S(1)}, u32[]{:S(2)}) copy-start(f32[788]{0:T(1024)S(1)} %broadcast_multiply_fusion.36) | copy-start | bytes 9460
  166.4 54.1 %copy-start.346 = (f32[788]{0:T(1024)}, f32[788]{0:T(1024)S(1)}, u32[]{:S(2)}) copy-start(f32[788]{0:T(1024)S(1)} %broadcast_multiply_fusion.35) | copy-start | bytes 9460
  170.9 45.7 %copy-start.348 = (f32[788]{0:T(1024)}, f32[788]{0:T(1024)S(1)}, u32[]{:S(2)}) copy-start(f32[788]{0:T(1024)S(1)} %broadcast_multiply_fusion.34) | copy-start | bytes 9460
  183.4 4.9 copy-start.356
  188.3 5.6 copy-start.523
  189.8 12.2 %slice-start = ((s8[9437184]{0:T(1024)(128)(4,1)}), s8[1048576]{0:T(1024)(128)(4,1)S(1)}, s32[]{:S(2)}) async-start(s8[9437184]{0:T(1024)(128)(4,1)} %bitcast.1128), calls=%async_computation.6 | async-start | bytes 2097152
  203.8 5.4 slice-start.3
  324.5 4.8 copy-start.307
  329.3 5.2 copy-start.146
  329.3 5.2 copy-start.367
  388.9 189.1 %reduce-scatter.7.cloned.1.call-start = ((), (), s32[]{:S(2)}) async-start(), calls=%async_computation.4 | async-start | bytes 13369344 | tf_op jit(solution)/shard_map/reduce_scatter | solution.py:88
  468.5 223.0 %all-gather.4.cloned.1.call-start = ((), (), s32[]{:S(2)}) async-start(), calls=%async_computation.3 | async-start | bytes 26738688 | tf_op jit(solution)/shard_map/all_gather | solution.py:100
  487.1 310.4 %all-gather.6.cloned.1.call-start = ((), (), s32[]{:S(2)}) async-start(), calls=%async_computation.5 | async-start | bytes 26738688 | tf_op jit(solution)/shard_map/all_gather | solution.py:101
  493.4 88.8 %copy-start.309 = (f32[4,1000]{1,0:T(4,128)S(1)}, f32[4,1000]{1,0:T(4,128)}, u32[]{:S(2)}) copy-start(f32[4,1000]{1,0:T(4,128)} %copy-done.308) | copy-start | bytes 48004
  493.4 88.8 %copy-start.360 = (f32[4,192]{1,0:T(4,128)S(1)}, f32[4,192]{1,0:T(4,128)}, u32[]{:S(2)}) copy-start(f32[4,192]{1,0:T(4,128)} %copy-done.359) | copy-start | bytes 9220
  493.4 88.9 %copy-start.515 = (f32[4]{0:T(128)S(1)}, f32[4]{0:T(128)}, u32[]{:S(2)}) copy-start(f32[4]{0:T(128)} %copy-done.514) | copy-start | bytes 52
  493.4 88.9 %copy-start.517 = (f32[4]{0:T(128)S(1)}, f32[4]{0:T(128)}, u32[]{:S(2)}) copy-start(f32[4]{0:T(128)} %copy-done.516) | copy-start | bytes 52
  493.4 88.9 %copy-start.519 = (f32[4]{0:T(128)S(1)}, f32[4]{0:T(128)}, u32[]{:S(2)}) copy-start(f32[4]{0:T(128)} %copy-done.518) | copy-start | bytes 52
  493.4 88.9 %copy-start.521 = (f32[4]{0:T(128)S(1)}, f32[4]{0:T(128)}, u32[]{:S(2)}) copy-start(f32[4]{0:T(128)} %copy-done.520) | copy-start | bytes 52
  493.5 88.9 %copy-start.524 = (s32[4]{0:T(128)S(1)}, s32[4]{0:T(128)}, u32[]{:S(2)}) copy-start(s32[4]{0:T(128)} %param.13) | copy-start | bytes 52
  582.2 48.7 %copy-start.87 = (bf16[4,197,192]{1,2,0:T(8,128)(2,1)S(1)}, bf16[4,197,192]{1,2,0:T(8,128)(2,1)}, u32[]{:S(2)}) copy-start(bf16[4,197,192]{1,2,0:T(8,128)(2,1)} %param.12) | copy-start | bytes 907780
  619.2 16.5 %collective-permute-start = (bf16[16,1000]{1,0:T(8,128)(2,1)S(1)}, bf16[16,1000]{1,0:T(8,128)(2,1)S(1)}, u32[]{:S(2)}, u32[]{:S(2)}) collective-permute-start(bf16[16,1000]{1,0:T(8,128)(2,1)S(1)} %fusion), channel_id=1, source_target_pairs={{0,1},{1,2},{2,3},{3,4},{4,5},{5,6},{6,7},{7,8},{8,9},{9,10},{10,1... | collective-permute-start | bytes 96008
  620.5 15.2 %collective-permute-start.1 = (bf16[16,1000]{1,0:T(8,128)(2,1)S(1)}, bf16[16,1000]{1,0:T(8,128)(2,1)}, u32[]{:S(2)}, u32[]{:S(2)}) collective-permute-start(bf16[16,1000]{1,0:T(8,128)(2,1)S(1)} %fusion), channel_id=1, source_target_pairs={{0,2},{1,3},{2,4},{3,5},{4,6},{5,7},{6,8},{7,9},{8,10},{9,11},{10,... | collective-permute-start | bytes 96008
  622.4 13.3 %collective-permute-start.2 = (bf16[16,1000]{1,0:T(8,128)(2,1)S(1)}, bf16[16,1000]{1,0:T(8,128)(2,1)}, u32[]{:S(2)}, u32[]{:S(2)}) collective-permute-start(bf16[16,1000]{1,0:T(8,128)(2,1)S(1)} %fusion), channel_id=1, source_target_pairs={{0,3},{1,4},{2,5},{3,6},{4,7},{5,8},{6,9},{7,10},{8,11},{9,12},{10... | collective-permute-start | bytes 96008
  624.9 10.8 %collective-permute-start.3 = (bf16[12,1000]{1,0:T(8,128)(2,1)}, bf16[12,1000]{1,0:T(8,128)(2,1)}, u32[]{:S(2)}, u32[]{:S(2)}) collective-permute-start(bf16[12,1000]{1,0:T(8,128)(2,1)} %slice.703), channel_id=1, source_target_pairs={{0,4},{1,5},{2,6},{3,7},{4,8},{5,9},{6,10},{7,11},{8,12},{9,13},{1... | collective-permute-start | bytes 72008
  633.1 30.9 %copy-start.88 = (f32[32,192,48]{1,0,2:T(8,128)S(1)}, f32[32,192,48]{1,0,2:T(8,128)}, u32[]{:S(2)}) copy-start(f32[32,192,48]{1,0,2:T(8,128)} %get-tuple-element.36) | copy-start | bytes 3538948
  820.4 10.3 %copy-start.306 = (f32[788,192]{0,1:T(8,128)S(1)}, f32[788,192]{0,1:T(8,128)}, u32[]{:S(2)}) copy-start(f32[788,192]{0,1:T(8,128)} %reshape.1263) | copy-start | bytes 1815556
  (491 other events, 994.5 us)
Sparse Core Ops, SparseCore 0:
  389.0 93.2 reduce-scatter.4
  487.5 90.4 reduce-scatter.6
  580.2 111.2 all-gather.3
  694.2 103.3 all-gather.5
where the time goes:
time: 937 us; the launch traced here: 920 us
  matrix products  394 us (42%)
  waiting for transfers between devices  187 us (20%)
  local copies, waits for them, and re-layouts  172 us (18%)
  other arithmetic  78 us (8%)
  blocking collectives  53.8 us (6%)
  between operations  23.1 us (2%)
  starting transfers between devices  11.6 us (1%)
    dot_general x64, matrix products, block_forward(): jnp.dot(gelu_out, down_w, preferred_element_type=jnp.float32)  151 us
    reduce_scatter x1, waiting for transfers between devices, local_step(): lax.psum_scatter(down_grad, 'data', scatter_dimension=1, tiled=True)  84.5 us
    all_gather x1, waiting for transfers between devices, local_step(): new_w_down = lax.all_gather(down_part, 'data', axis=1, tiled=True)  73.3 us
    unnamed x1069, local copies, waits for them, and re-layouts  70.9 us
    dot_general x31, matrix products, backward_layers(): lax.dot_general(grad_rows, down_b[layer], CONTRACT_LAST, preferred_elemen...  61.9 us
    dot_general x32, matrix products, backward_layers(): lax.dot_general(gelu_out, grad_rows, CONTRACT_ROWS, preferred_element_typ...  60.7 us
    dot_general x32, matrix products, block_forward(): jnp.dot(u_rows, up_w, preferred_element_type=jnp.float32)  49.4 us
    dot_general x32, matrix products, backward_layers(): lax.dot_general(u_rows, grad_pre, CONTRACT_ROWS, preferred_element_type=j...  45.9 us
  transfers between devices with their start and end apart: 8, of which 4 were waited for; matrix products, arithmetic and copies ran while one was open for 21% of the time, Pallas kernels for 0%

commit v1 on v0

v1 whole, which is shorter than its diff:
```python
import functools

import jax
import jax.numpy as jnp
from jax import lax
from jax.experimental import pallas as pl
from jax.experimental.pallas import tpu as pltpu
from jax.sharding import PartitionSpec as P

LN_EPS = 1e-6
GELU_C = 0.7978845608028654
GELU_A = 0.044715
F32 = jnp.float32
BF16 = jnp.bfloat16
LAST = (((1,), (1,)), ((), ()))
ROWS = (((0,), (0,)), ((), ()))
MESH_ID = pl.DeviceIdType.MESH
VMEM_LIMIT = 62 * 1024 * 1024
CHUNKS = 5
SLOTS = 4
AG_SLOTS = 8
PARTS = 3
ORDER = ((0, 1, 2), (1, 2, 0), (2, 0, 1))


def norm_parts(values):
    mean_v = jnp.mean(values, axis=-1, keepdims=True)
    centered = values - mean_v
    var_v = jnp.mean(centered * centered, axis=-1, keepdims=True)
    return centered, lax.rsqrt(var_v + LN_EPS)


def norm_pull(normed, scale, grad):
    mean_g = jnp.mean(grad, axis=-1, keepdims=True)
    mean_gn = jnp.mean(grad * normed, axis=-1, keepdims=True)
    return scale * (grad - mean_g - normed * mean_gn)


def gelu(values):
    half = 0.5 * values
    tanh_v = jnp.tanh(values * (GELU_C + (GELU_C * GELU_A) * (values * values)))
    return half + half * tanh_v


def gelu_both(values):
    half = 0.5 * values
    square = values * values
    tanh_v = jnp.tanh(values * (GELU_C + (GELU_C * GELU_A) * square))
    out = half + half * tanh_v
    slope = (0.5 + 0.5 * tanh_v) + (half * (1.0 - tanh_v * tanh_v)) * (GELU_C + (3.0 * GELU_C * GELU_A) * square)
    return out, slope


def pack_rows(x_ref, wide, rows, n_img, n_tok):
    wide[...] = jnp.zeros_like(wide)
    for img in range(n_img):
        wide[img * n_tok : (img + 1) * n_tok, :] = x_ref[img].astype(F32)
    rows[...] = wide[...].astype(BF16)


def pool_mask(shape, n_img, n_tok, row_axis):
    row = lax.broadcasted_iota(jnp.int32, shape, row_axis)
    img = lax.broadcasted_iota(jnp.int32, shape, 1 - row_axis)
    inside = (row >= img * n_tok) & (row < (img + 1) * n_tok) & (img < n_img)
    return jnp.where(inside, 1.0, 0.0).astype(BF16)


def pooled_norm(rows, n_img, n_tok):
    n_rows = rows.shape[0]
    mask = pool_mask((8, n_rows), n_img, n_tok, 1)
    pooled = jnp.dot(mask, rows[...], preferred_element_type=F32) * (1.0 / n_tok)
    centered, scale = norm_parts(pooled)
    return centered * scale, scale


def forward_kernel(n_img, n_tok, batch_total, n_cls, x_ref, lab_ref, wu_ref, wd_ref, wh_ref, xs_ref, pre_ref, grad_ref, norm_ref, gl_ref, wide, rows):
    layer = pl.program_id(0)

    @pl.when(layer == 0)
    def _():
        pack_rows(x_ref, wide, rows, n_img, n_tok)

    up_b = wu_ref[0].astype(BF16)
    down_b = wd_ref[0].astype(BF16)
    step = rows.shape[0] // CHUNKS
    for chunk in range(CHUNKS):
        sl = slice(chunk * step, (chunk + 1) * step)
        x_rows = rows[sl, :]
        xs_ref[0, sl, :] = x_rows
        x_wide = x_rows.astype(F32)
        centered, scale = norm_parts(x_wide)
        u_rows = (centered * scale).astype(BF16)
        pre = jnp.dot(u_rows, up_b, preferred_element_type=F32).astype(BF16)
        pre_ref[0, sl, :] = pre
        z_rows = gelu(pre.astype(F32)).astype(BF16)
        y_rows = jnp.dot(z_rows, down_b, preferred_element_type=F32).astype(BF16)
        rows[sl, :] = (x_wide + y_rows.astype(F32)).astype(BF16)

    @pl.when(layer == pl.num_programs(0) - 1)
    def _():
        normed, scale = pooled_norm(rows, n_img, n_tok)
        normed_b = normed.astype(BF16)
        head_b = wh_ref[...].astype(BF16)
        logits = jnp.dot(normed_b, head_b, preferred_element_type=F32)
        top = jnp.max(logits, axis=-1, keepdims=True)
        exps = jnp.exp(logits - top)
        probs = exps / jnp.sum(exps, axis=-1, keepdims=True)
        classes = lax.broadcasted_iota(jnp.int32, logits.shape, 1)
        image = lax.broadcasted_iota(jnp.int32, logits.shape, 0)
        targets = jnp.where(classes == lab_ref[...], 1.0, 0.0)
        grad_logits = jnp.where(image < n_img, (probs - targets) * (1.0 / batch_total), 0.0)
        grad_b = grad_logits.astype(BF16)
        gl_ref[...] = grad_b
        norm_ref[...] = normed_b
        grad_normed = lax.dot_general(grad_b, head_b, LAST, preferred_element_type=F32).astype(BF16)
        grad_pooled = norm_pull(normed, scale, grad_normed.astype(F32))
        per_row = (grad_pooled / n_tok).astype(BF16)
        spread = pool_mask((rows.shape[0], 8), n_img, n_tok, 0)
        grad_ref[...] = jnp.dot(spread, per_row, preferred_element_type=F32).astype(BF16)


def next_kernel(n_img, n_tok, lr_ref, x_ref, wu_ref, wd_ref, mom_ref, wh_ref, nwu_ref, nwd_ref, log_ref, wide, rows):
    layer = pl.program_id(0)

    @pl.when(layer == 0)
    def _():
        pack_rows(x_ref, wide, rows, n_img, n_tok)

    rate = lr_ref[0, 0]
    up_a = mom_ref[0, 0].T.astype(F32)
    mixed = mom_ref[0, 2]
    up_z = mixed.T.astype(F32)[64:, :]
    nwu_ref[0, :128, :] = wu_ref[0, :128, :] - rate * up_a
    nwu_ref[0, 128:, :] = wu_ref[0, 128:, :] - rate * up_z
    nwd_ref[0, :, :128] = wd_ref[0, :, :128] - rate * mom_ref[0, 1].astype(F32)
    nwd_ref[0, :, 128:] = wd_ref[0, :, 128:] - rate * mixed[:, :64].astype(F32)
    up_b = nwu_ref[0].astype(BF16)
    down_b = nwd_ref[0].astype(BF16)
    step = rows.shape[0] // CHUNKS
    for chunk in range(CHUNKS):
        sl = slice(chunk * step, (chunk + 1) * step)
        x_wide = rows[sl, :].astype(F32)
        centered, scale = norm_parts(x_wide)
        u_rows = (centered * scale).astype(BF16)
        pre = jnp.dot(u_rows, up_b, preferred_element_type=F32).astype(BF16)
        z_rows = gelu(pre.astype(F32)).astype(BF16)
        y_rows = jnp.dot(z_rows, down_b, preferred_element_type=F32).astype(BF16)
        rows[sl, :] = (x_wide + y_rows.astype(F32)).astype(BF16)

    @pl.when(layer == pl.num_programs(0) - 1)
    def _():
        normed, _ = pooled_norm(rows, n_img, n_tok)
        log_ref[...] = jnp.dot(normed.astype(BF16), wh_ref[...].astype(BF16), preferred_element_type=F32)


def backward_kernel(
    n_items, sc_ref, gh_ref, grad_ref, xs_ref, pre_ref, wu_ref, wd_ref, mom_ref, nm_ref, all_ref,
    g_rows, z_buf, da_buf, u_buf, g_buf, pair_buf, sum_buf, rcv0, rcv1, rcv2, ag_buf,
    d2d_send, d2d_recv, rs_send, rs_recv, ag_send, ag_recv, out_sem,
):
    t = pl.program_id(0)
    me = lax.axis_index("data")
    core = me % 2
    place = ((me // 8) % 2, (me // 4) % 2, (me // 2) % 2)
    peers = tuple(me + (1 - 2 * place[axis]) * w for axis, w in ((0, 8), (1, 4), (2, 2)))
    twin = me + 1 - 2 * core
    rcv = (rcv0, rcv1, rcv2)

    @pl.when(t == 0)
    def _():
        barrier = pltpu.get_barrier_semaphore()
        for peer in peers + (twin,):
            pl.semaphore_signal(barrier, inc=1, device_id=(peer,), device_id_type=MESH_ID)
        pl.semaphore_wait(barrier, 4)

    def pair_copy(item):
        return pltpu.make_async_remote_copy(
            src_ref=g_buf.at[item % SLOTS, :, :, :, :, 1 - core],
            dst_ref=pair_buf.at[item % SLOTS],
            send_sem=d2d_send.at[0, item % 2],
            recv_sem=d2d_recv.at[0, item % 2],
            device_id=(twin,),
            device_id_type=MESH_ID,
        )

    def cut(part, stage, value):
        index = [slice(None)] * 3
        for axis in ORDER[part][:stage]:
            index[axis] = place[axis]
        index[ORDER[part][stage]] = value
        return tuple(index)

    def rs_copy(item, stage, part):
        axis = ORDER[part][stage]
        return pltpu.make_async_remote_copy(
            src_ref=sum_buf.at[(item % SLOTS, part) + cut(part, stage, 1 - place[axis])],
            dst_ref=rcv[stage].at[item % SLOTS, part],
            send_sem=rs_send.at[stage, part, item % 2],
            recv_sem=rs_recv.at[stage, part, item % 2],
            device_id=(peers[axis],),
            device_id_type=MESH_ID,
        )

    def ag_copy(item, stage, part):
        index = [place[0], place[1], place[2]]
        for axis in ORDER[part][:stage]:
            index[axis] = slice(None)
        view = ag_buf.at[(item % AG_SLOTS, part) + tuple(index) + (core,)]
        return pltpu.make_async_remote_copy(
            src_ref=view,
            dst_ref=view,
            send_sem=ag_send.at[stage, part, item % 2],
            recv_sem=ag_recv.at[stage, part, item % 2],
            device_id=(peers[ORDER[part][stage]],),
            device_id_type=MESH_ID,
        )

    def twin_copy(item):
        view = ag_buf.at[item % AG_SLOTS, :, :, :, :, core]
        return pltpu.make_async_remote_copy(
            src_ref=view,
            dst_ref=view,
            send_sem=d2d_send.at[1, item % 2],
            recv_sem=d2d_recv.at[1, item % 2],
            device_id=(twin,),
            device_id_type=MESH_ID,
        )

    def out_copy(item):
        return pltpu.make_async_copy(ag_buf.at[item % AG_SLOTS], all_ref.at[n_items - 1 - item], out_sem.at[item % 2])

    def at_lag(lag):
        return (t >= lag) & (t < n_items + lag)

    @pl.when(t == 1)
    def _():
        g_rows[...] = grad_ref[...]

    @pl.when((t >= 1) & (t < n_items))
    def _():
        up_b = wu_ref[0].astype(BF16)
        down_b = wd_ref[0].astype(BF16)
        step = g_rows.shape[0] // CHUNKS
        grad_old = g_rows[...]
        for chunk in range(CHUNKS):
            sl = slice(chunk * step, (chunk + 1) * step)
            g_old = grad_old[sl, :]
            z_wide, slope = gelu_both(pre_ref[0, sl, :].astype(F32))
            z_buf[sl, :] = z_wide.astype(BF16)
            grad_z = lax.dot_general(g_old, down_b, LAST, preferred_element_type=F32).astype(BF16)
            grad_a = (grad_z.astype(F32) * slope).astype(BF16)
            da_buf[sl, :] = grad_a
            centered, scale = norm_parts(xs_ref[0, sl, :].astype(F32))
            normed = centered * scale
            u_buf[sl, :] = normed.astype(BF16)
            grad_u = lax.dot_general(grad_a, up_b, LAST, preferred_element_type=F32).astype(BF16)
            grad_x = norm_pull(normed, scale, grad_u.astype(F32))
            g_rows[sl, :] = (g_old.astype(F32) + grad_x).astype(BF16)
        down_t = lax.dot_general(grad_old, z_buf[...], ROWS, preferred_element_type=F32).astype(BF16)
        up_g = lax.dot_general(u_buf[...], da_buf[...], ROWS, preferred_element_type=F32).astype(BF16)
        z_buf[:128, :] = up_g[:128, :]
        z_buf[128:256, :] = down_t[:128, :]
        z_buf[256:320, :] = down_t[128:, :]
        z_buf[320:384, :] = up_g[128:, :]

    @pl.when(at_lag(9))
    def _():
        out_copy(t - 9).wait()

    @pl.when(at_lag(8))
    def _():
        item = t - 8
        twin_copy(item).wait()
        out_copy(item).start()

    @pl.when(at_lag(7))
    def _():
        item = t - 7
        for part in range(PARTS):
            ag_copy(item, 2, part).wait()
        twin_copy(item).start()

    for stage in (1, 0):

        @pl.when(at_lag(5 + stage))
        def _(stage=stage):
            item = t - 5 - stage
            for part in range(PARTS):
                ag_copy(item, stage, part).wait()
                ag_copy(item, stage + 1, part).start()

    @pl.when(at_lag(4))
    def _():
        item = t - 4
        for part in range(PARTS):
            rs_copy(item, 2, part).wait()
            grad = sum_buf[item % SLOTS, part, place[0], place[1], place[2]].astype(F32) + rcv[2][item % SLOTS, part].astype(F32)
            grad = grad.astype(BF16).astype(F32)
            mom = sc_ref[0, 0] * mom_ref[0, part] + grad
            nm_ref[0, part] = mom
            ag_buf[item % AG_SLOTS, part, place[0], place[1], place[2], core] = mom.astype(BF16)
            ag_copy(item, 0, part).start()

    for stage in (1, 0):

        @pl.when(at_lag(2 + stage))
        def _(stage=stage):
            item = t - 2 - stage
            for part in range(PARTS):
                rs_copy(item, stage, part).wait()
                kept = (item % SLOTS, part) + cut(part, stage, place[ORDER[part][stage]])
                both = sum_buf[kept].astype(F32) + rcv[stage][item % SLOTS, part].astype(F32)
                sum_buf[kept] = both.astype(BF16)
                rs_copy(item, stage + 1, part).start()

    @pl.when(at_lag(1))
    def _():
        item = t - 1
        pair_copy(item).wait()
        for part in range(PARTS):
            both = g_buf[item % SLOTS, part, :, :, :, core].astype(F32) + pair_buf[item % SLOTS, part].astype(F32)
            sum_buf[item % SLOTS, part] = both.astype(BF16)
            rs_copy(item, 0, part).start()

    @pl.when(t == 0)
    def _():
        g_buf[0] = gh_ref[...]
        pair_copy(0).start()

    @pl.when((t >= 1) & (t < n_items))
    def _():
        for part in range(PARTS):
            turned = z_buf[part * 128 : (part + 1) * 128, :].T
            for dev in range(16):
                block = turned[dev * 48 : (dev + 1) * 48, :]
                g_buf[t % SLOTS, part, dev // 8, (dev // 4) % 2, (dev // 2) % 2, dev % 2] = block
        pair_copy(t).start()


def whole(shape):
    return pl.BlockSpec(shape, lambda i: (0,) * len(shape))


def solution(mesh):
    n_dev = mesh.shape["data"]

    def local_step(x_now, x_next, labels, w_up, w_down, w_head, mom_up, mom_down, mom_head, learn_rate, mom_decay):
        n_img, n_tok, width = x_now.shape
        n_layers, _, hidden = w_up.shape
        n_cls = w_head.shape[1]
        n_rows = -(-n_img * n_tok // (16 * CHUNKS)) * 16 * CHUNKS
        n_items = n_layers + 1
        cols = mom_up.shape[2]
        head_rows = mom_head.shape[0]
        n_tile = -(-n_cls // 128)
        head_each = head_rows * n_tile // PARTS

        lab = jnp.pad(labels, (0, 8 - n_img)).reshape(8, 1)
        xs, pre, grad_rows, normed, grad_logits = pl.pallas_call(
            functools.partial(forward_kernel, n_img, n_tok, n_img * n_dev, n_cls),
            grid=(n_layers,),
            in_specs=[
                whole(x_now.shape),
                whole((8, 1)),
                pl.BlockSpec((1, width, hidden), lambda i: (i, 0, 0)),
                pl.BlockSpec((1, hidden, width), lambda i: (i, 0, 0)),
                whole(w_head.shape),
            ],
            out_specs=[
                pl.BlockSpec((1, n_rows, width), lambda i: (i, 0, 0)),
                pl.BlockSpec((1, n_rows, hidden), lambda i: (i, 0, 0)),
                whole((n_rows, width)),
                whole((8, width)),
                whole((8, n_cls)),
            ],
            out_shape=[
                jax.ShapeDtypeStruct((n_layers, n_rows, width), BF16),
                jax.ShapeDtypeStruct((n_layers, n_rows, hidden), BF16),
                jax.ShapeDtypeStruct((n_rows, width), BF16),
                jax.ShapeDtypeStruct((8, width), BF16),
                jax.ShapeDtypeStruct((8, n_cls), BF16),
            ],
            scratch_shapes=[pltpu.VMEM((n_rows, width), F32), pltpu.VMEM((n_rows, width), BF16)],
            compiler_params=pltpu.CompilerParams(vmem_limit_bytes=VMEM_LIMIT),
            name="step_forward",
        )(x_now, lab, w_up, w_down, w_head)

        def head_blocks(values):
            n_part = values.shape[0] // head_rows
            wide = jnp.pad(values, ((0, 0), (0, n_tile * 128 - n_cls)))
            blocks = wide.reshape(n_part, PARTS, head_each, 128)
            return jnp.pad(blocks, ((0, 0), (0, 0), (0, cols - head_each), (0, 0)))

        head_grad = lax.dot_general(normed, grad_logits, ROWS, preferred_element_type=F32).astype(BF16)
        head_g = head_blocks(head_grad).transpose(1, 0, 2, 3).reshape(PARTS, 2, 2, 2, 2, cols, 128)
        up_t = mom_up.transpose(0, 2, 1)
        mom_in = jnp.stack(
            [up_t[:, :, :128], mom_down[:, :, :128], jnp.concatenate([mom_down[:, :, 128:], up_t[:, :, 128:]], axis=2)], axis=1
        )
        mom_in = jnp.concatenate([mom_in, head_blocks(mom_head)], axis=0)

        def layer_at(t):
            return jnp.clip(n_items - 1 - t, 0, n_layers - 1)

        def update_at(t):
            return n_items - 1 - jnp.clip(t - 4, 0, n_items - 1)

        block = (SLOTS, PARTS, 2, 2, 2)
        new_mom, gathered = pl.pallas_call(
            functools.partial(backward_kernel, n_items),
            grid=(n_items + 9,),
            in_specs=[
                pl.BlockSpec(memory_space=pltpu.SMEM),
                whole((PARTS, 2, 2, 2, 2, cols, 128)),
                whole((n_rows, width)),
                pl.BlockSpec((1, n_rows, width), lambda t: (layer_at(t), 0, 0)),
                pl.BlockSpec((1, n_rows, hidden), lambda t: (layer_at(t), 0, 0)),
                pl.BlockSpec((1, width, hidden), lambda t: (layer_at(t), 0, 0)),
                pl.BlockSpec((1, hidden, width), lambda t: (layer_at(t), 0, 0)),
                pl.BlockSpec((1, PARTS, cols, 128), lambda t: (update_at(t), 0, 0, 0)),
            ],
            out_specs=[
                pl.BlockSpec((1, PARTS, cols, 128), lambda t: (update_at(t), 0, 0, 0)),
                pl.BlockSpec(memory_space=pl.ANY),
            ],
            out_shape=[
                jax.ShapeDtypeStruct((n_items, PARTS, cols, 128), F32),
                jax.ShapeDtypeStruct((n_items, PARTS, 2, 2, 2, 2, cols, 128), BF16),
            ],
            scratch_shapes=[
                pltpu.VMEM((n_rows, width), BF16),
                pltpu.VMEM((n_rows, hidden), BF16),
                pltpu.VMEM((n_rows, hidden), BF16),
                pltpu.VMEM((n_rows, width), BF16),
                pltpu.VMEM(block + (2, cols, 128), BF16),
                pltpu.VMEM(block + (cols, 128), BF16),
                pltpu.VMEM(block + (cols, 128), BF16),
                pltpu.VMEM((SLOTS, PARTS, 2, 2, cols, 128), BF16),
                pltpu.VMEM((SLOTS, PARTS, 2, cols, 128), BF16),
                pltpu.VMEM((SLOTS, PARTS, cols, 128), BF16),
                pltpu.VMEM((AG_SLOTS, PARTS, 2, 2, 2, 2, cols, 128), BF16),
                pltpu.SemaphoreType.DMA((2, 2)),
                pltpu.SemaphoreType.DMA((2, 2)),
                pltpu.SemaphoreType.DMA((3, PARTS, 2)),
                pltpu.SemaphoreType.DMA((3, PARTS, 2)),
                pltpu.SemaphoreType.DMA((3, PARTS, 2)),
                pltpu.SemaphoreType.DMA((3, PARTS, 2)),
                pltpu.SemaphoreType.DMA((2,)),
            ],
            compiler_params=pltpu.CompilerParams(vmem_limit_bytes=VMEM_LIMIT, collective_id=0, has_side_effects=True),
            name="step_backward",
        )(mom_decay.reshape(1, 1), head_g, grad_rows, xs, pre, w_up, w_down, mom_in)

        gathered = gathered.reshape(n_items, PARTS, n_dev * cols, 128)
        head_all = gathered[n_layers].reshape(PARTS, n_dev, cols, 128)[:, :, :head_each]
        head_all = head_all.transpose(1, 0, 2, 3).reshape(n_dev * head_rows, n_tile * 128)[:, :n_cls]
        new_w_head = w_head - learn_rate * head_all.astype(F32)

        new_w_up, new_w_down, logits = pl.pallas_call(
            functools.partial(next_kernel, n_img, n_tok),
            grid=(n_layers,),
            in_specs=[
                pl.BlockSpec(memory_space=pltpu.SMEM),
                whole(x_next.shape),
                pl.BlockSpec((1, width, hidden), lambda i: (i, 0, 0)),
                pl.BlockSpec((1, hidden, width), lambda i: (i, 0, 0)),
                pl.BlockSpec((1, PARTS, n_dev * cols, 128), lambda i: (i, 0, 0, 0)),
                whole(w_head.shape),
            ],
            out_specs=[
                pl.BlockSpec((1, width, hidden), lambda i: (i, 0, 0)),
                pl.BlockSpec((1, hidden, width), lambda i: (i, 0, 0)),
                whole((8, n_cls)),
            ],
            out_shape=[
                jax.ShapeDtypeStruct(w_up.shape, F32),
                jax.ShapeDtypeStruct(w_down.shape, F32),
                jax.ShapeDtypeStruct((8, n_cls), F32),
            ],
            scratch_shapes=[pltpu.VMEM((n_rows, width), F32), pltpu.VMEM((n_rows, width), BF16)],
            compiler_params=pltpu.CompilerParams(vmem_limit_bytes=VMEM_LIMIT),
            name="step_next",
        )(learn_rate.reshape(1, 1), x_next, w_up, w_down, gathered, new_w_head)

        layers = new_mom[:n_layers]
        new_mom_down = jnp.concatenate([layers[:, 1], layers[:, 2, :, :64]], axis=2)
        new_mom_up = jnp.concatenate([layers[:, 0], layers[:, 2, :, 64:]], axis=2).transpose(0, 2, 1)
        new_mom_head = new_mom[n_layers][:, :head_each].reshape(head_rows, n_tile * 128)[:, :n_cls]
        return (logits[:n_img], new_w_up, new_w_down, new_w_head, new_mom_up, new_mom_down, new_mom_head)

    spec_up = P(None, None, "data")
    spec_down = P(None, "data", None)
    spec_head = P("data", None)
    return jax.shard_map(
        local_step,
        mesh=mesh,
        in_specs=(P("data"), P("data"), P("data"), P(), P(), P(), spec_up, spec_down, spec_head, P(), P()),
        out_specs=(P("data"), P(), P(), P(), spec_up, spec_down, spec_head),
        check_vma=False,
    )
```

time: 937 us -> 362 us (0.39); the launches traced: 920 us -> 358 us
  matrix products: 394 us -> 1.16 us
  Pallas kernels: 0 us -> 293 us
  waiting for transfers between devices: 187 us -> 0 us
  local copies, waits for them, and re-layouts: 172 us -> 55.8 us
  other arithmetic: 78 us -> 5.46 us
  blocking collectives: 53.8 us -> 0 us
  between operations: 23.1 us -> 2.1 us
  starting transfers between devices: 11.6 us -> 0 us
    dot_general x226 -> x1, matrix products: 394 us -> 1.16 us  [local_step(): lax.dot_general(normed, grad_logits, ROWS, preferred_element_type=F32)]
    pallas_call x0 -> x3, Pallas kernels: none -> 293 us  [the longest x1 171 us: local_step(): pl.pallas_call(functools.partial(backward_kernel, n_items), grid=(n_items...]
    all_gather x2 -> x0, waiting for transfers between devices: 96.8 us -> none  [the longest x1 73.3 us: local_step(): new_w_down = lax.all_gather(down_part, 'data', axis=1, tiled=True)]
    reduce_scatter x2 -> x0, waiting for transfers between devices: 90.5 us -> none  [the longest x1 84.5 us: local_step(): lax.psum_scatter(down_grad, 'data', scatter_dimension=1, tiled=True)]
    convert_element_type x38 -> x0, other arithmetic: 48.3 us -> none  [the longest x1 10.3 us: local_step(): new_w_down.astype(jnp.bfloat16)]
    all_gather x2 -> x0, local copies, waits for them, and re-layouts: 45.7 us -> none  [the longest x1 22.8 us: local_step(): new_w_up = lax.all_gather(up_part, 'data', axis=2, tiled=True)]
    unnamed x1 -> x0, blocking collectives: 36.5 us -> none
    another operation x2 -> x1, local copies, waits for them, and re-layouts: 34.7 us -> 0.05 us  [local_step(): jnp.stack([up_t[:, :, :128], mom_down[:, :, :128], jnp.concatenate([mom_d...]
  transfers between devices with their start and end apart: 8 -> 0, of which waited for: 4 -> 0; matrix products, arithmetic and copies ran while one was open for 21% -> 0% of each run, Pallas kernels for 0% -> 0%
where the time goes in v1:
time: 362 us; the launch traced here: 358 us
  Pallas kernels  293 us (81%)
  local copies, waits for them, and re-layouts  55.8 us (15%)
  other arithmetic  5.46 us (2%)
    pallas_call x1, Pallas kernels, local_step(): pl.pallas_call(functools.partial(backward_kernel, n_items), grid=(n_items...  171 us
    pallas_call x1, Pallas kernels, local_step(): pl.pallas_call(functools.partial(next_kernel, n_img, n_tok), grid=(n_laye...  62.1 us
    pallas_call x1, Pallas kernels, local_step(): pl.pallas_call(functools.partial(forward_kernel, n_img, n_tok, n_img * n_...  60.2 us
    unnamed x24, local copies, waits for them, and re-layouts  48.2 us

profile of v1, /device:TPU:0, one launch (start us, length us, event | category | flops | bytes accessed | tf_op | source)
XLA Modules:
  0.0 358.0 jit_solution(3910172812367823864)
XLA Ops:
  0.6 0.0 copy-start.5
  0.6 0.0 copy-start.9
  0.7 22.1 %copy.26.wd_ref = f32[32,768,192]{2,1,0:T(8,128)} copy(f32[32,768,192]{1,2,0:T(8,128)} %param.15) | data formatting | bytes 37748736 | tf_op args[4]
  22.7 0.0 copy-done.5
  22.7 1.0 copy.18.x_ref
  23.7 0.0 copy-done.9
  23.7 0.7 copy.19.lab_ref
  24.4 60.2 %step_forward.1 = (bf16[32,800,192]{2,1,0:T(8,128)(2,1)}, bf16[32,800,768]{2,1,0:T(8,128)(2,1)}, bf16[800,192]{1,0:T(8,128)(2,1)}, bf16[8,192]{1,0:T(8,128)(2,1)}, bf16[8,1000]{1,0:T(8,128)(2,1)}) custom-call(bf16[4,197,192]{2,1,0:T(8,128)(2,1)} %copy.18.x_ref, s32[8,1]{1,0:T(8,128)} %copy.19.lab_ref, f32[32,192,768]{2,1,0:T(8,128)} %wu_ref.5, ...), custom_call_target="tpu_custom_call" | custom-call | tf_op jit(solution)/shard_map/step_forward/pallas_call | solution.py:359
  84.6 0.0 copy-start.3
  84.6 1.2 convolution_convert_fusion
  85.8 0.2 reshape.46
  86.0 0.0 slice-start
  86.0 0.0 copy-start.4
  86.0 0.9 pad.22
  86.9 0.0 copy-done.3
  86.9 0.1 slice.67
  87.0 0.0 copy-start.1
  87.0 0.4 slice-done
  87.3 0.5 copy-done.4
  87.9 0.0 copy-start.7
  87.9 0.3 slice_bitcast_fusion
  88.2 0.4 copy-done.1
  88.6 0.1 slice_bitcast_fusion.5
  88.6 0.2 copy-done.7
  88.8 1.6 select_maximum_fusion.mom_ref
  91.1 171.1 %step_backward.1 = (f32[33,3,48,128]{3,2,1,0:T(8,128)}, bf16[33,3,2,2,2,2,48,128]{7,6,5,4,3,2,1,0:T(8,128)(2,1)}) custom-call(f32[1,1]{1,0:T(1,128)} %bitcast.38.sc_ref, bf16[3,2,2,2,2,48,128]{6,5,4,3,2,1,0:T(8,128)(2,1)} %bitcast.40, bf16[800,192]{1,0:T(8,128)(2,1)} %get-tuple-element.19.grad_ref, bf16[32,800,192]{2,1,0:T(8,128)(2,1)} %get-tuple-element.20.xs_ref, ...), custom_call_target="tpu_custom_call" | custom-call | tf_op jit(solution)/shard_map/step_backward/pallas_call | solution.py:409
  262.3 0.0 copy-start
  262.3 1.6 slice_bitcast_fusion.2
  263.9 0.5 copy-done
  264.5 0.3 slice_bitcast_fusion.1
  264.7 1.3 pad_maximum_fusion
  266.0 0.0 copy-start.2
  266.0 1.3 maximum_bitcast_fusion
  267.3 0.0 copy-start.6
  267.3 1.2 slice.55
  268.5 0.2 reshape.50
  269.3 0.0 copy-done.2
  269.3 1.0 multiply_subtract_fusion.wh_ref
  270.3 0.0 copy-done.6
  270.3 1.0 copy.25.x_ref
  271.3 62.1 %step_next.1 = (f32[32,192,768]{2,1,0:T(8,128)}, f32[32,768,192]{2,1,0:T(8,128)}, f32[8,1000]{1,0:T(8,128)}) custom-call(f32[1,1]{1,0:T(1,128)} %bitcast.37.lr_ref, bf16[4,197,192]{2,1,0:T(8,128)(2,1)} %copy.25.x_ref, f32[32,192,768]{2,1,0:T(8,128)} %wu_ref.5, f32[32,768,192]{2,1,0:T(8,128)} %copy.26.wd_ref, bf16[33,3,768,128]{3,2,1,0:T(8,128)(2,1)} %bitcast.39, ...), custom_call_target="tpu_custom_call" | custom-call | tf_op jit(solution)/shard_map/step_next/pallas_call | solution.py:459
  333.4 0.0 copy-start.8
  333.4 22.5 %copy.27 = f32[32,768,192]{1,2,0:T(8,128)} copy(f32[32,768,192]{2,1,0:T(8,128)} %get-tuple-element.29) | data formatting | bytes 37748736
  355.8 0.0 copy-done.8
  355.8 0.6 slice.58
  356.5 0.9 slice_bitcast_fusion.6
  357.4 0.6 reshape.51
  (7 shorter events, 0.1 us)
Async XLA Ops:
  0.6 22.1 %copy-start.5 = (bf16[4,197,192]{1,2,0:T(8,128)(2,1)S(1)}, bf16[4,197,192]{1,2,0:T(8,128)(2,1)}, u32[]{:S(2)}) copy-start(bf16[4,197,192]{1,2,0:T(8,128)(2,1)} %param.11) | copy-start | bytes 907780
  0.6 23.1 %copy-start.9 = (s32[4]{0:T(128)S(1)}, s32[4]{0:T(128)}, u32[]{:S(2)}) copy-start(s32[4]{0:T(128)} %param.13) | copy-start | bytes 52
  84.6 2.3 copy-start.3
  86.0 1.4 slice-start
  86.0 1.9 copy-start.4
  87.0 1.6 copy-start.1
  87.9 1.0 copy-start.7
  262.3 2.2 copy-start
  266.0 3.3 copy-start.2
  267.3 3.0 copy-start.6
  333.4 22.5 %copy-start.8 = (f32[8,1000]{1,0:T(8,128)S(1)}, f32[8,1000]{1,0:T(8,128)}, u32[]{:S(2)}) copy-start(f32[8,1000]{1,0:T(8,128)} %get-tuple-element.23) | copy-start | bytes 96004

commit v2 on v1

--- a/solution.py
+++ b/solution.py
@@ -37,24 +37,22 @@
 
 
 def gelu(values):
-    half = 0.5 * values
-    tanh_v = jnp.tanh(values * (GELU_C + (GELU_C * GELU_A) * (values * values)))
-    return half + half * tanh_v
+    inner = values * (GELU_C + (GELU_C * GELU_A) * (values * values))
+    return values * (0.5 + 0.5 * jnp.tanh(inner))
 
 
 def gelu_both(values):
-    half = 0.5 * values
     square = values * values
-    tanh_v = jnp.tanh(values * (GELU_C + (GELU_C * GELU_A) * square))
-    out = half + half * tanh_v
-    slope = (0.5 + 0.5 * tanh_v) + (half * (1.0 - tanh_v * tanh_v)) * (GELU_C + (3.0 * GELU_C * GELU_A) * square)
+    share = 0.5 + 0.5 * jnp.tanh(values * (GELU_C + (GELU_C * GELU_A) * square))
+    out = values * share
+    slope = share + (out * (1.0 - share)) * (2.0 * GELU_C + (6.0 * GELU_C * GELU_A) * square)
     return out, slope
 
 
 def pack_rows(x_ref, wide, rows, n_img, n_tok):
     wide[...] = jnp.zeros_like(wide)
     for img in range(n_img):
-        wide[img * n_tok : (img + 1) * n_tok, :] = x_ref[img].astype(F32)
+        wide[img * n_tok : (img + 1) * n_tok, :] = x_ref[img].astype(F32).T
     rows[...] = wide[...].astype(BF16)
 
 
@@ -80,21 +78,22 @@
     def _():
         pack_rows(x_ref, wide, rows, n_img, n_tok)
 
-    up_b = wu_ref[0].astype(BF16)
-    down_b = wd_ref[0].astype(BF16)
     step = rows.shape[0] // CHUNKS
-    for chunk in range(CHUNKS):
-        sl = slice(chunk * step, (chunk + 1) * step)
-        x_rows = rows[sl, :]
-        xs_ref[0, sl, :] = x_rows
-        x_wide = x_rows.astype(F32)
-        centered, scale = norm_parts(x_wide)
-        u_rows = (centered * scale).astype(BF16)
-        pre = jnp.dot(u_rows, up_b, preferred_element_type=F32).astype(BF16)
-        pre_ref[0, sl, :] = pre
-        z_rows = gelu(pre.astype(F32)).astype(BF16)
-        y_rows = jnp.dot(z_rows, down_b, preferred_element_type=F32).astype(BF16)
-        rows[sl, :] = (x_wide + y_rows.astype(F32)).astype(BF16)
+    for sub in range(wu_ref.shape[0]):
+        up_b = wu_ref[sub].astype(BF16)
+        down_b = wd_ref[sub].astype(BF16)
+        for chunk in range(CHUNKS):
+            sl = slice(chunk * step, (chunk + 1) * step)
+            x_rows = rows[sl, :]
+            xs_ref[sub, sl, :] = x_rows
+            x_wide = x_rows.astype(F32)
+            centered, scale = norm_parts(x_wide)
+            u_rows = (centered * scale).astype(BF16)
+            pre = jnp.dot(u_rows, up_b, preferred_element_type=F32).astype(BF16)
+            pre_ref[sub, sl, :] = pre
+            z_rows = gelu(pre.astype(F32)).astype(BF16)
+            y_rows = lax.dot_general(z_rows, down_b, LAST, preferred_element_type=F32).astype(BF16)
+            rows[sl, :] = (x_wide + y_rows.astype(F32)).astype(BF16)
 
     @pl.when(layer == pl.num_programs(0) - 1)
     def _():
@@ -127,25 +126,24 @@
         pack_rows(x_ref, wide, rows, n_img, n_tok)
 
     rate = lr_ref[0, 0]
-    up_a = mom_ref[0, 0].T.astype(F32)
-    mixed = mom_ref[0, 2]
-    up_z = mixed.T.astype(F32)[64:, :]
-    nwu_ref[0, :128, :] = wu_ref[0, :128, :] - rate * up_a
-    nwu_ref[0, 128:, :] = wu_ref[0, 128:, :] - rate * up_z
-    nwd_ref[0, :, :128] = wd_ref[0, :, :128] - rate * mom_ref[0, 1].astype(F32)
-    nwd_ref[0, :, 128:] = wd_ref[0, :, 128:] - rate * mixed[:, :64].astype(F32)
-    up_b = nwu_ref[0].astype(BF16)
-    down_b = nwd_ref[0].astype(BF16)
     step = rows.shape[0] // CHUNKS
-    for chunk in range(CHUNKS):
-        sl = slice(chunk * step, (chunk + 1) * step)
-        x_wide = rows[sl, :].astype(F32)
-        centered, scale = norm_parts(x_wide)
-        u_rows = (centered * scale).astype(BF16)
-        pre = jnp.dot(u_rows, up_b, preferred_element_type=F32).astype(BF16)
-        z_rows = gelu(pre.astype(F32)).astype(BF16)
-        y_rows = jnp.dot(z_rows, down_b, preferred_element_type=F32).astype(BF16)
-        rows[sl, :] = (x_wide + y_rows.astype(F32)).astype(BF16)
+    for sub in range(wu_ref.shape[0]):
+        mixed = mom_ref[sub, 2].T.astype(F32)
+        nwu_ref[sub, :128, :] = wu_ref[sub, :128, :] - rate * mom_ref[sub, 0].T.astype(F32)
+        nwu_ref[sub, 128:, :] = wu_ref[sub, 128:, :] - rate * mixed[64:, :]
+        nwd_ref[sub, :128, :] = wd_ref[sub, :128, :] - rate * mom_ref[sub, 1].T.astype(F32)
+        nwd_ref[sub, 128:, :] = wd_ref[sub, 128:, :] - rate * mixed[:64, :]
+        up_b = nwu_ref[sub].astype(BF16)
+        down_b = nwd_ref[sub].astype(BF16)
+        for chunk in range(CHUNKS):
+            sl = slice(chunk * step, (chunk + 1) * step)
+            x_wide = rows[sl, :].astype(F32)
+            centered, scale = norm_parts(x_wide)
+            u_rows = (centered * scale).astype(BF16)
+            pre = jnp.dot(u_rows, up_b, preferred_element_type=F32).astype(BF16)
+            z_rows = gelu(pre.astype(F32)).astype(BF16)
+            y_rows = lax.dot_general(z_rows, down_b, LAST, preferred_element_type=F32).astype(BF16)
+            rows[sl, :] = (x_wide + y_rows.astype(F32)).astype(BF16)
 
     @pl.when(layer == pl.num_programs(0) - 1)
     def _():
@@ -154,7 +152,7 @@
 
 
 def backward_kernel(
-    n_items, sc_ref, gh_ref, grad_ref, xs_ref, pre_ref, wu_ref, wd_ref, mom_ref, nm_ref, all_ref,
+    n_items, sc_ref, gh_ref, grad_ref, xs_ref, pre_ref, wu_ref, wd_ref, mh_ref, mu_ref, md_ref, nmh_ref, nmu_ref, nmd_ref, all_ref,
     g_rows, z_buf, da_buf, u_buf, g_buf, pair_buf, sum_buf, rcv0, rcv1, rcv2, ag_buf,
     d2d_send, d2d_recv, rs_send, rs_recv, ag_send, ag_recv, out_sem,
 ):
@@ -247,7 +245,7 @@
             g_old = grad_old[sl, :]
             z_wide, slope = gelu_both(pre_ref[0, sl, :].astype(F32))
             z_buf[sl, :] = z_wide.astype(BF16)
-            grad_z = lax.dot_general(g_old, down_b, LAST, preferred_element_type=F32).astype(BF16)
+            grad_z = jnp.dot(g_old, down_b, preferred_element_type=F32).astype(BF16)
             grad_a = (grad_z.astype(F32) * slope).astype(BF16)
             da_buf[sl, :] = grad_a
             centered, scale = norm_parts(xs_ref[0, sl, :].astype(F32))
@@ -258,10 +256,11 @@
             g_rows[sl, :] = (g_old.astype(F32) + grad_x).astype(BF16)
         down_t = lax.dot_general(grad_old, z_buf[...], ROWS, preferred_element_type=F32).astype(BF16)
         up_g = lax.dot_general(u_buf[...], da_buf[...], ROWS, preferred_element_type=F32).astype(BF16)
-        z_buf[:128, :] = up_g[:128, :]
-        z_buf[128:256, :] = down_t[:128, :]
-        z_buf[256:320, :] = down_t[128:, :]
-        z_buf[320:384, :] = up_g[128:, :]
+        for part, value in enumerate((up_g[:128, :], down_t[:128, :], jnp.concatenate([down_t[128:, :], up_g[128:, :]], axis=0))):
+            turned = value.T
+            for dev in range(16):
+                block = turned[dev * 48 : (dev + 1) * 48, :]
+                g_buf[t % SLOTS, part, dev // 8, (dev // 4) % 2, (dev // 2) % 2, dev % 2] = block
 
     @pl.when(at_lag(9))
     def _():
@@ -294,12 +293,35 @@
         item = t - 4
         for part in range(PARTS):
             rs_copy(item, 2, part).wait()
-            grad = sum_buf[item % SLOTS, part, place[0], place[1], place[2]].astype(F32) + rcv[2][item % SLOTS, part].astype(F32)
-            grad = grad.astype(BF16).astype(F32)
-            mom = sc_ref[0, 0] * mom_ref[0, part] + grad
-            nm_ref[0, part] = mom
+
+        def reduced(part):
+            return (sum_buf[item % SLOTS, part, place[0], place[1], place[2]] + rcv[2][item % SLOTS, part]).astype(F32)
+
+        def hand_on(part, mom):
             ag_buf[item % AG_SLOTS, part, place[0], place[1], place[2], core] = mom.astype(BF16)
             ag_copy(item, 0, part).start()
+
+        @pl.when(t == 4)
+        def _():
+            for part in range(PARTS):
+                mom = sc_ref[0, 0] * mh_ref[part] + reduced(part)
+                nmh_ref[part] = mom
+                hand_on(part, mom)
+
+        @pl.when(t > 4)
+        def _():
+            mixed = reduced(2)
+            up_a = sc_ref[0, 0] * mu_ref[0, :, :128] + reduced(0)
+            down_a = sc_ref[0, 0] * md_ref[0, :, :128] + reduced(1)
+            up_z = sc_ref[0, 0] * mu_ref[0, :, 128:] + mixed[:, 64:]
+            down_z = sc_ref[0, 0] * md_ref[0, :, 128:] + mixed[:, :64]
+            nmu_ref[0, :, :128] = up_a
+            nmu_ref[0, :, 128:] = up_z
+            nmd_ref[0, :, :128] = down_a
+            nmd_ref[0, :, 128:] = down_z
+            hand_on(0, up_a)
+            hand_on(1, down_a)
+            hand_on(2, jnp.concatenate([down_z, up_z], axis=1))
 
     for stage in (1, 0):
 
@@ -309,8 +331,7 @@
             for part in range(PARTS):
                 rs_copy(item, stage, part).wait()
                 kept = (item % SLOTS, part) + cut(part, stage, place[ORDER[part][stage]])
-                both = sum_buf[kept].astype(F32) + rcv[stage][item % SLOTS, part].astype(F32)
-                sum_buf[kept] = both.astype(BF16)
+                sum_buf[kept] = sum_buf[kept] + rcv[stage][item % SLOTS, part]
                 rs_copy(item, stage + 1, part).start()
 
     @pl.when(at_lag(1))
@@ -318,8 +339,7 @@
         item = t - 1
         pair_copy(item).wait()
         for part in range(PARTS):
-            both = g_buf[item % SLOTS, part, :, :, :, core].astype(F32) + pair_buf[item % SLOTS, part].astype(F32)
-            sum_buf[item % SLOTS, part] = both.astype(BF16)
+            sum_buf[item % SLOTS, part] = g_buf[item % SLOTS, part, :, :, :, core] + pair_buf[item % SLOTS, part]
             rs_copy(item, 0, part).start()
 
     @pl.when(t == 0)
@@ -329,11 +349,6 @@
 
     @pl.when((t >= 1) & (t < n_items))
     def _():
-        for part in range(PARTS):
-            turned = z_buf[part * 128 : (part + 1) * 128, :].T
-            for dev in range(16):
-                block = turned[dev * 48 : (dev + 1) * 48, :]
-                g_buf[t % SLOTS, part, dev // 8, (dev // 4) % 2, (dev // 2) % 2, dev % 2] = block
         pair_copy(t).start()
 
 
@@ -355,20 +370,22 @@
         n_tile = -(-n_cls // 128)
         head_each = head_rows * n_tile // PARTS
 
+        down_t = w_down.transpose(0, 2, 1)
+        per = 2 if n_layers % 2 == 0 else 1
         lab = jnp.pad(labels, (0, 8 - n_img)).reshape(8, 1)
         xs, pre, grad_rows, normed, grad_logits = pl.pallas_call(
             functools.partial(forward_kernel, n_img, n_tok, n_img * n_dev, n_cls),
-            grid=(n_layers,),
+            grid=(n_layers // per,),
             in_specs=[
-                whole(x_now.shape),
+                whole((n_img, width, n_tok)),
                 whole((8, 1)),
-                pl.BlockSpec((1, width, hidden), lambda i: (i, 0, 0)),
-                pl.BlockSpec((1, hidden, width), lambda i: (i, 0, 0)),
+                pl.BlockSpec((per, width, hidden), lambda i: (i, 0, 0)),
+                pl.BlockSpec((per, width, hidden), lambda i: (i, 0, 0)),
                 whole(w_head.shape),
             ],
             out_specs=[
-                pl.BlockSpec((1, n_rows, width), lambda i: (i, 0, 0)),
-                pl.BlockSpec((1, n_rows, hidden), lambda i: (i, 0, 0)),
+                pl.BlockSpec((per, n_rows, width), lambda i: (i, 0, 0)),
+                pl.BlockSpec((per, n_rows, hidden), lambda i: (i, 0, 0)),
                 whole((n_rows, width)),
                 whole((8, width)),
                 whole((8, n_cls)),
@@ -383,7 +400,7 @@
             scratch_shapes=[pltpu.VMEM((n_rows, width), F32), pltpu.VMEM((n_rows, width), BF16)],
             compiler_params=pltpu.CompilerParams(vmem_limit_bytes=VMEM_LIMIT),
             name="step_forward",
-        )(x_now, lab, w_up, w_down, w_head)
+        )(x_now.transpose(0, 2, 1), lab, w_up, down_t, w_head)
 
         def head_blocks(values):
             n_part = values.shape[0] // head_rows
@@ -393,20 +410,14 @@
 
         head_grad = lax.dot_general(normed, grad_logits, ROWS, preferred_element_type=F32).astype(BF16)
         head_g = head_blocks(head_grad).transpose(1, 0, 2, 3).reshape(PARTS, 2, 2, 2, 2, cols, 128)
-        up_t = mom_up.transpose(0, 2, 1)
-        mom_in = jnp.stack(
-            [up_t[:, :, :128], mom_down[:, :, :128], jnp.concatenate([mom_down[:, :, 128:], up_t[:, :, 128:]], axis=2)], axis=1
-        )
-        mom_in = jnp.concatenate([mom_in, head_blocks(mom_head)], axis=0)
-
         def layer_at(t):
             return jnp.clip(n_items - 1 - t, 0, n_layers - 1)
 
         def update_at(t):
-            return n_items - 1 - jnp.clip(t - 4, 0, n_items - 1)
+            return n_items - 1 - jnp.clip(t - 4, 1, n_items - 1)
 
         block = (SLOTS, PARTS, 2, 2, 2)
-        new_mom, gathered = pl.pallas_call(
+        mom_head_new, mom_up_new, new_mom_down, gathered = pl.pallas_call(
             functools.partial(backward_kernel, n_items),
             grid=(n_items + 9,),
             in_specs=[
@@ -416,15 +427,21 @@
                 pl.BlockSpec((1, n_rows, width), lambda t: (layer_at(t), 0, 0)),
                 pl.BlockSpec((1, n_rows, hidden), lambda t: (layer_at(t), 0, 0)),
                 pl.BlockSpec((1, width, hidden), lambda t: (layer_at(t), 0, 0)),
-                pl.BlockSpec((1, hidden, width), lambda t: (layer_at(t), 0, 0)),
-                pl.BlockSpec((1, PARTS, cols, 128), lambda t: (update_at(t), 0, 0, 0)),
+                pl.BlockSpec((1, width, hidden), lambda t: (layer_at(t), 0, 0)),
+                whole((PARTS, cols, 128)),
+                pl.BlockSpec((1, cols, width), lambda t: (update_at(t), 0, 0)),
+                pl.BlockSpec((1, cols, width), lambda t: (update_at(t), 0, 0)),
             ],
             out_specs=[
-                pl.BlockSpec((1, PARTS, cols, 128), lambda t: (update_at(t), 0, 0, 0)),
+                whole((PARTS, cols, 128)),
+                pl.BlockSpec((1, cols, width), lambda t: (update_at(t), 0, 0)),
+                pl.BlockSpec((1, cols, width), lambda t: (update_at(t), 0, 0)),
                 pl.BlockSpec(memory_space=pl.ANY),
             ],
             out_shape=[
-                jax.ShapeDtypeStruct((n_items, PARTS, cols, 128), F32),
+                jax.ShapeDtypeStruct((PARTS, cols, 128), F32),
+                jax.ShapeDtypeStruct((n_layers, cols, width), F32),
+                jax.ShapeDtypeStruct((n_layers, cols, width), F32),
                 jax.ShapeDtypeStruct((n_items, PARTS, 2, 2, 2, 2, cols, 128), BF16),
             ],
             scratch_shapes=[
@@ -449,44 +466,41 @@
             ],
             compiler_params=pltpu.CompilerParams(vmem_limit_bytes=VMEM_LIMIT, collective_id=0, has_side_effects=True),
             name="step_backward",
-        )(mom_decay.reshape(1, 1), head_g, grad_rows, xs, pre, w_up, w_down, mom_in)
+        )(mom_decay.reshape(1, 1), head_g, grad_rows, xs, pre, w_up, down_t, head_blocks(mom_head)[0], mom_up.transpose(0, 2, 1), mom_down)
 
         gathered = gathered.reshape(n_items, PARTS, n_dev * cols, 128)
         head_all = gathered[n_layers].reshape(PARTS, n_dev, cols, 128)[:, :, :head_each]
         head_all = head_all.transpose(1, 0, 2, 3).reshape(n_dev * head_rows, n_tile * 128)[:, :n_cls]
         new_w_head = w_head - learn_rate * head_all.astype(F32)
 
-        new_w_up, new_w_down, logits = pl.pallas_call(
+        new_w_up, new_down_t, logits = pl.pallas_call(
             functools.partial(next_kernel, n_img, n_tok),
-            grid=(n_layers,),
+            grid=(n_layers // per,),
             in_specs=[
                 pl.BlockSpec(memory_space=pltpu.SMEM),
-                whole(x_next.shape),
-                pl.BlockSpec((1, width, hidden), lambda i: (i, 0, 0)),
-                pl.BlockSpec((1, hidden, width), lambda i: (i, 0, 0)),
-                pl.BlockSpec((1, PARTS, n_dev * cols, 128), lambda i: (i, 0, 0, 0)),
+                whole((n_img, width, n_tok)),
+                pl.BlockSpec((per, width, hidden), lambda i: (i, 0, 0)),
+                pl.BlockSpec((per, width, hidden), lambda i: (i, 0, 0)),
+                pl.BlockSpec((per, PARTS, n_dev * cols, 128), lambda i: (i, 0, 0, 0)),
                 whole(w_head.shape),
             ],
             out_specs=[
-                pl.BlockSpec((1, width, hidden), lambda i: (i, 0, 0)),
-                pl.BlockSpec((1, hidden, width), lambda i: (i, 0, 0)),
+                pl.BlockSpec((per, width, hidden), lambda i: (i, 0, 0)),
+                pl.BlockSpec((per, width, hidden), lambda i: (i, 0, 0)),
                 whole((8, n_cls)),
             ],
             out_shape=[
                 jax.ShapeDtypeStruct(w_up.shape, F32),
-                jax.ShapeDtypeStruct(w_down.shape, F32),
+                jax.ShapeDtypeStruct(w_up.shape, F32),
                 jax.ShapeDtypeStruct((8, n_cls), F32),
             ],
             scratch_shapes=[pltpu.VMEM((n_rows, width), F32), pltpu.VMEM((n_rows, width), BF16)],
             compiler_params=pltpu.CompilerParams(vmem_limit_bytes=VMEM_LIMIT),
             name="step_next",
-        )(learn_rate.reshape(1, 1), x_next, w_up, w_down, gathered, new_w_head)
-
-        layers = new_mom[:n_layers]
-        new_mom_down = jnp.concatenate([layers[:, 1], layers[:, 2, :, :64]], axis=2)
-        new_mom_up = jnp.concatenate([layers[:, 0], layers[:, 2, :, 64:]], axis=2).transpose(0, 2, 1)
-        new_mom_head = new_mom[n_layers][:, :head_each].reshape(head_rows, n_tile * 128)[:, :n_cls]
-        return (logits[:n_img], new_w_up, new_w_down, new_w_head, new_mom_up, new_mom_down, new_mom_head)
+        )(learn_rate.reshape(1, 1), x_next.transpose(0, 2, 1), w_up, down_t, gathered, new_w_head)
+
+        new_mom_head = mom_head_new[:, :head_each].reshape(head_rows, n_tile * 128)[:, :n_cls]
+        return (logits[:n_img], new_w_up, new_down_t.transpose(0, 2, 1), new_w_head, mom_up_new.transpose(0, 2, 1), new_mom_down, new_mom_head)
 
     spec_up = P(None, None, "data")
     spec_down = P(None, "data", None)

time: 362 us -> 286 us (0.79); the launches traced: 358 us -> 286 us
  local copies, waits for them, and re-layouts: 55.8 us -> 10.2 us
  Pallas kernels: 293 us -> 271 us
  other arithmetic: 5.46 us -> 1 us
    unnamed x24 -> x10, local copies, waits for them, and re-layouts: 48.2 us -> 3.81 us
    pallas_call x1, Pallas kernels: 171 us -> 163 us  [local_step(): pl.pallas_call(functools.partial(backward_kernel, n_items), grid=(n_items...]
    pallas_call x1, Pallas kernels: 60.2 us -> 52.4 us  [local_step(): pl.pallas_call(functools.partial(forward_kernel, n_img, n_tok, n_img * n_...]
    pallas_call x1, Pallas kernels: 62.1 us -> 56.3 us  [local_step(): pl.pallas_call(functools.partial(next_kernel, n_img, n_tok), grid=(n_laye...]
where the time goes in v2:
time: 286 us
  Pallas kernels  271 us (95%)
  local copies, waits for them, and re-layouts  10.2 us (4%)
    pallas_call x1, Pallas kernels, local_step(): pl.pallas_call(functools.partial(backward_kernel, n_items), grid=(n_items...  163 us
    pallas_call x1, Pallas kernels, local_step(): pl.pallas_call(functools.partial(next_kernel, n_img, n_tok), grid=(n_laye...  56.3 us
    pallas_call x1, Pallas kernels, local_step(): pl.pallas_call(functools.partial(forward_kernel, n_img, n_tok, n_img * n_...  52.4 us

profile of v2, /device:TPU:0, one launch (start us, length us, event | category | flops | bytes accessed | tf_op | source)
XLA Modules:
  0.0 285.8 jit_solution(12110525589484338032)
XLA Ops:
  0.6 0.7 pad_bitcast_fusion.1
  1.3 0.7 copy.18.lab_ref
  2.0 0.0 copy-start.2
  2.0 52.4 %step_forward.1 = (bf16[32,800,192]{2,1,0:T(8,128)(2,1)}, bf16[32,800,768]{2,1,0:T(8,128)(2,1)}, bf16[800,192]{1,0:T(8,128)(2,1)}, bf16[8,192]{1,0:T(8,128)(2,1)}, bf16[8,1000]{1,0:T(8,128)(2,1)}) custom-call(bf16[4,192,197]{2,1,0:T(8,128)(2,1)} %bitcast.34, s32[8,1]{1,0:T(8,128)} %copy.18.lab_ref, f32[32,192,768]{2,1,0:T(8,128)} %wu_ref.5, ...), custom_call_target="tpu_custom_call" | custom-call | tf_op jit(solution)/shard_map/step_forward/pallas_call | solution.py:376
  54.4 1.0 convolution_convert_fusion
  55.5 0.2 reshape.46
  55.7 0.9 pad.22
  56.6 0.0 copy-done.2
  56.6 0.6 pad_bitcast_fusion.mh_ref
  57.9 0.0 copy-start
  57.9 162.7 %step_backward.1 = (f32[3,48,128]{2,1,0:T(8,128)}, f32[32,48,192]{2,1,0:T(8,128)}, f32[32,48,192]{2,1,0:T(8,128)}, bf16[33,3,2,2,2,2,48,128]{7,6,5,4,3,2,1,0:T(8,128)(2,1)}) custom-call(f32[1,1]{1,0:T(1,128)} %bitcast.25.sc_ref, bf16[3,2,2,2,2,48,128]{6,5,4,3,2,1,0:T(8,128)(2,1)} %bitcast.30, bf16[800,192]{1,0:T(8,128)(2,1)} %get-tuple-element.21.grad_ref, ...), custom_call_target="tpu_custom_call" | custom-call | tf_op jit(solution)/shard_map/step_backward/pallas_call | solution.py:420
  220.6 1.1 slice.19
  221.8 0.2 reshape.50
  222.6 0.0 copy-done
  222.6 1.0 multiply_subtract_fusion.wh_ref
  223.6 0.0 copy-start.3
  223.6 0.0 copy-start.1
  223.6 56.3 %step_next.1 = (f32[32,192,768]{2,1,0:T(8,128)}, f32[32,192,768]{2,1,0:T(8,128)}, f32[8,1000]{1,0:T(8,128)}) custom-call(f32[1,1]{1,0:T(1,128)} %bitcast.24.lr_ref, bf16[4,192,197]{2,1,0:T(8,128)(2,1)} %bitcast.35, f32[32,192,768]{2,1,0:T(8,128)} %wu_ref.5, f32[32,192,768]{2,1,0:T(8,128)} %bitcast.28, bf16[33,3,768,128]{3,2,1,0:T(8,128)(2,1)} %bitcast.29, ...), custom_call_target="tpu_custom_call" | custom-call | tf_op jit(solution)/shard_map/step_next/pallas_call | solution.py:476
  279.9 1.4 slice.22
  281.3 0.0 copy-done.3
  281.3 0.6 reshape.51
  282.0 2.7 copy.27
  284.6 0.0 copy-done.1
  284.6 1.1 copy.28
  (6 shorter events, 0.1 us)
Async XLA Ops:
  2.0 54.6 %copy-start.2 = (f32[12,1000]{1,0:T(8,128)S(1)}, f32[12,1000]{1,0:T(8,128)}, u32[]{:S(2)}) copy-start(f32[12,1000]{1,0:T(8,128)} %param.19) | copy-start | bytes 144004
  57.9 164.7 %copy-start = (f32[192,1000]{1,0:T(8,128)S(1)}, f32[192,1000]{1,0:T(8,128)}, u32[]{:S(2)}) copy-start(f32[192,1000]{1,0:T(8,128)} %wh_ref.1) | copy-start | bytes 2304004
  223.6 57.7 %copy-start.3 = (f32[3,48,128]{2,1,0:T(8,128)S(1)}, f32[3,48,128]{2,1,0:T(8,128)}, u32[]{:S(2)}) copy-start(f32[3,48,128]{2,1,0:T(8,128)} %get-tuple-element.30) | copy-start | bytes 221188
  223.6 61.0 %copy-start.1 = (f32[32,48,192]{2,1,0:T(8,128)S(1)}, f32[32,48,192]{2,1,0:T(8,128)}, u32[]{:S(2)}) copy-start(f32[32,48,192]{2,1,0:T(8,128)} %get-tuple-element.43) | copy-start | bytes 3538948

commit v3 on v2

--- a/solution.py
+++ b/solution.py
@@ -15,10 +15,9 @@
 LAST = (((1,), (1,)), ((), ()))
 ROWS = (((0,), (0,)), ((), ()))
 MESH_ID = pl.DeviceIdType.MESH
-VMEM_LIMIT = 62 * 1024 * 1024
+VMEM_LIMIT = 66_000_000
 CHUNKS = 5
 SLOTS = 4
-AG_SLOTS = 8
 PARTS = 3
 ORDER = ((0, 1, 2), (1, 2, 0), (2, 0, 1))
 
@@ -118,51 +117,20 @@
         grad_ref[...] = jnp.dot(spread, per_row, preferred_element_type=F32).astype(BF16)
 
 
-def next_kernel(n_img, n_tok, lr_ref, x_ref, wu_ref, wd_ref, mom_ref, wh_ref, nwu_ref, nwd_ref, log_ref, wide, rows):
-    layer = pl.program_id(0)
-
-    @pl.when(layer == 0)
-    def _():
-        pack_rows(x_ref, wide, rows, n_img, n_tok)
-
-    rate = lr_ref[0, 0]
-    step = rows.shape[0] // CHUNKS
-    for sub in range(wu_ref.shape[0]):
-        mixed = mom_ref[sub, 2].T.astype(F32)
-        nwu_ref[sub, :128, :] = wu_ref[sub, :128, :] - rate * mom_ref[sub, 0].T.astype(F32)
-        nwu_ref[sub, 128:, :] = wu_ref[sub, 128:, :] - rate * mixed[64:, :]
-        nwd_ref[sub, :128, :] = wd_ref[sub, :128, :] - rate * mom_ref[sub, 1].T.astype(F32)
-        nwd_ref[sub, 128:, :] = wd_ref[sub, 128:, :] - rate * mixed[:64, :]
-        up_b = nwu_ref[sub].astype(BF16)
-        down_b = nwd_ref[sub].astype(BF16)
-        for chunk in range(CHUNKS):
-            sl = slice(chunk * step, (chunk + 1) * step)
-            x_wide = rows[sl, :].astype(F32)
-            centered, scale = norm_parts(x_wide)
-            u_rows = (centered * scale).astype(BF16)
-            pre = jnp.dot(u_rows, up_b, preferred_element_type=F32).astype(BF16)
-            z_rows = gelu(pre.astype(F32)).astype(BF16)
-            y_rows = lax.dot_general(z_rows, down_b, LAST, preferred_element_type=F32).astype(BF16)
-            rows[sl, :] = (x_wide + y_rows.astype(F32)).astype(BF16)
-
-    @pl.when(layer == pl.num_programs(0) - 1)
-    def _():
-        normed, _ = pooled_norm(rows, n_img, n_tok)
-        log_ref[...] = jnp.dot(normed.astype(BF16), wh_ref[...].astype(BF16), preferred_element_type=F32)
-
-
-def backward_kernel(
-    n_items, sc_ref, gh_ref, grad_ref, xs_ref, pre_ref, wu_ref, wd_ref, mh_ref, mu_ref, md_ref, nmh_ref, nmu_ref, nmd_ref, all_ref,
-    g_rows, z_buf, da_buf, u_buf, g_buf, pair_buf, sum_buf, rcv0, rcv1, rcv2, ag_buf,
-    d2d_send, d2d_recv, rs_send, rs_recv, ag_send, ag_recv, out_sem,
+def update_kernel(
+    n_items, n_img, n_tok, sc_ref, gh_ref, grad_ref, xs_ref, pre_ref, wu_ref, wd_ref, mh_ref, mu_ref, md_ref, x_ref,
+    nmh_ref, nmu_ref, nmd_ref, nwu_ref, nwd_ref, head_ref, norm_ref,
+    rows, z_buf, da_buf, u_buf, wide, g_buf, pair_buf, sum_buf, rcv0, rcv1, rcv2, all_buf,
+    d2d_send, d2d_recv, twin_send, twin_recv, rs_send, rs_recv, ag_send, ag_recv,
 ):
     t = pl.program_id(0)
     me = lax.axis_index("data")
-    core = me % 2
-    place = ((me // 8) % 2, (me // 4) % 2, (me // 2) % 2)
+    core = lax.rem(me, 2)
+    place = (lax.div(me, 8), lax.rem(lax.div(me, 4), 2), lax.rem(lax.div(me, 2), 2))
     peers = tuple(me + (1 - 2 * place[axis]) * w for axis, w in ((0, 8), (1, 4), (2, 2)))
     twin = me + 1 - 2 * core
     rcv = (rcv0, rcv1, rcv2)
+    last_update, n_early, n_late, first_next = ticks(n_items)
 
     @pl.when(t == 0)
     def _():
@@ -172,11 +140,12 @@
         pl.semaphore_wait(barrier, 4)
 
     def pair_copy(item):
+        slot = lax.rem(item, 2)
         return pltpu.make_async_remote_copy(
-            src_ref=g_buf.at[item % SLOTS, :, :, :, :, 1 - core],
-            dst_ref=pair_buf.at[item % SLOTS],
-            send_sem=d2d_send.at[0, item % 2],
-            recv_sem=d2d_recv.at[0, item % 2],
+            src_ref=g_buf.at[slot, :, :, :, :, 1 - core],
+            dst_ref=pair_buf.at[slot],
+            send_sem=d2d_send.at[slot],
+            recv_sem=d2d_recv.at[slot],
             device_id=(twin,),
             device_id_type=MESH_ID,
         )
@@ -190,56 +159,61 @@
 
     def rs_copy(item, stage, part):
         axis = ORDER[part][stage]
+        slot = lax.rem(item, 2)
         return pltpu.make_async_remote_copy(
-            src_ref=sum_buf.at[(item % SLOTS, part) + cut(part, stage, 1 - place[axis])],
-            dst_ref=rcv[stage].at[item % SLOTS, part],
-            send_sem=rs_send.at[stage, part, item % 2],
-            recv_sem=rs_recv.at[stage, part, item % 2],
+            src_ref=sum_buf.at[(lax.rem(item, SLOTS), part) + cut(part, stage, 1 - place[axis])],
+            dst_ref=rcv[stage].at[slot, part],
+            send_sem=rs_send.at[stage, part, slot],
+            recv_sem=rs_recv.at[stage, part, slot],
             device_id=(peers[axis],),
             device_id_type=MESH_ID,
         )
 
-    def ag_copy(item, stage, part):
+    def launched(tick):
+        even = lax.rem(tick, 2) == 0
+        early = (tick >= 4) & (tick < 4 + 2 * n_early) & even
+        late = (tick >= last_update - 1) & (tick <= last_update + n_late)
+        order = jnp.where(tick == last_update - 1, n_items - 2, jnp.where(tick == last_update, n_items - 1, n_items - 2 + last_update - tick))
+        return jnp.where(tick < last_update - 1, lax.div(tick - 4, 2), order), early | late
+
+    def ag_copy(tick, item, stage, part):
         index = [place[0], place[1], place[2]]
         for axis in ORDER[part][:stage]:
             index[axis] = slice(None)
-        view = ag_buf.at[(item % AG_SLOTS, part) + tuple(index) + (core,)]
+        view = all_buf.at[(item, part) + tuple(index) + (core,)]
         return pltpu.make_async_remote_copy(
             src_ref=view,
             dst_ref=view,
-            send_sem=ag_send.at[stage, part, item % 2],
-            recv_sem=ag_recv.at[stage, part, item % 2],
+            send_sem=ag_send.at[stage, part, lax.rem(tick, 4)],
+            recv_sem=ag_recv.at[stage, part, lax.rem(tick, 4)],
             device_id=(peers[ORDER[part][stage]],),
             device_id_type=MESH_ID,
         )
 
-    def twin_copy(item):
-        view = ag_buf.at[item % AG_SLOTS, :, :, :, :, core]
+    def twin_copy(tick, item):
+        view = all_buf.at[item, :, :, :, :, core]
         return pltpu.make_async_remote_copy(
             src_ref=view,
             dst_ref=view,
-            send_sem=d2d_send.at[1, item % 2],
-            recv_sem=d2d_recv.at[1, item % 2],
+            send_sem=twin_send.at[lax.rem(tick, 4)],
+            recv_sem=twin_recv.at[lax.rem(tick, 4)],
             device_id=(twin,),
             device_id_type=MESH_ID,
         )
 
-    def out_copy(item):
-        return pltpu.make_async_copy(ag_buf.at[item % AG_SLOTS], all_ref.at[n_items - 1 - item], out_sem.at[item % 2])
-
     def at_lag(lag):
         return (t >= lag) & (t < n_items + lag)
 
     @pl.when(t == 1)
     def _():
-        g_rows[...] = grad_ref[...]
+        rows[...] = grad_ref[...]
 
     @pl.when((t >= 1) & (t < n_items))
     def _():
         up_b = wu_ref[0].astype(BF16)
         down_b = wd_ref[0].astype(BF16)
-        step = g_rows.shape[0] // CHUNKS
-        grad_old = g_rows[...]
+        step = rows.shape[0] // CHUNKS
+        grad_old = rows[...]
         for chunk in range(CHUNKS):
             sl = slice(chunk * step, (chunk + 1) * step)
             g_old = grad_old[sl, :]
@@ -253,40 +227,30 @@
             u_buf[sl, :] = normed.astype(BF16)
             grad_u = lax.dot_general(grad_a, up_b, LAST, preferred_element_type=F32).astype(BF16)
             grad_x = norm_pull(normed, scale, grad_u.astype(F32))
-            g_rows[sl, :] = (g_old.astype(F32) + grad_x).astype(BF16)
+            rows[sl, :] = (g_old.astype(F32) + grad_x).astype(BF16)
         down_t = lax.dot_general(grad_old, z_buf[...], ROWS, preferred_element_type=F32).astype(BF16)
         up_g = lax.dot_general(u_buf[...], da_buf[...], ROWS, preferred_element_type=F32).astype(BF16)
         for part, value in enumerate((up_g[:128, :], down_t[:128, :], jnp.concatenate([down_t[128:, :], up_g[128:, :]], axis=0))):
             turned = value.T
             for dev in range(16):
                 block = turned[dev * 48 : (dev + 1) * 48, :]
-                g_buf[t % SLOTS, part, dev // 8, (dev // 4) % 2, (dev // 2) % 2, dev % 2] = block
-
-    @pl.when(at_lag(9))
-    def _():
-        out_copy(t - 9).wait()
-
-    @pl.when(at_lag(8))
-    def _():
-        item = t - 8
-        twin_copy(item).wait()
-        out_copy(item).start()
-
-    @pl.when(at_lag(7))
-    def _():
-        item = t - 7
-        for part in range(PARTS):
-            ag_copy(item, 2, part).wait()
-        twin_copy(item).start()
-
-    for stage in (1, 0):
-
-        @pl.when(at_lag(5 + stage))
-        def _(stage=stage):
-            item = t - 5 - stage
+                g_buf[lax.rem(t, 2), part, dev // 8, (dev // 4) % 2, (dev // 2) % 2, dev % 2] = block
+
+    for stage in (4, 3, 2, 1):
+        item, busy = launched(t - stage)
+
+        @pl.when(busy)
+        def _(stage=stage, item=item):
+            tick = t - stage
+            if stage == 4:
+                twin_copy(tick, item).wait()
+                return
             for part in range(PARTS):
-                ag_copy(item, stage, part).wait()
-                ag_copy(item, stage + 1, part).start()
+                ag_copy(tick, item, stage - 1, part).wait()
+                if stage < 3:
+                    ag_copy(tick, item, stage, part).start()
+            if stage == 3:
+                twin_copy(tick, item).start()
 
     @pl.when(at_lag(4))
     def _():
@@ -295,11 +259,10 @@
             rs_copy(item, 2, part).wait()
 
         def reduced(part):
-            return (sum_buf[item % SLOTS, part, place[0], place[1], place[2]] + rcv[2][item % SLOTS, part]).astype(F32)
+            return (sum_buf[lax.rem(item, SLOTS), part, place[0], place[1], place[2]] + rcv[2][lax.rem(item, 2), part]).astype(F32)
 
         def hand_on(part, mom):
-            ag_buf[item % AG_SLOTS, part, place[0], place[1], place[2], core] = mom.astype(BF16)
-            ag_copy(item, 0, part).start()
+            all_buf[item, part, place[0], place[1], place[2], core] = mom.astype(BF16)
 
         @pl.when(t == 4)
         def _():
@@ -323,6 +286,13 @@
             hand_on(1, down_a)
             hand_on(2, jnp.concatenate([down_z, up_z], axis=1))
 
+    item, busy = launched(t)
+
+    @pl.when(busy)
+    def _():
+        for part in range(PARTS):
+            ag_copy(t, item, 0, part).start()
+
     for stage in (1, 0):
 
         @pl.when(at_lag(2 + stage))
@@ -330,8 +300,8 @@
             item = t - 2 - stage
             for part in range(PARTS):
                 rs_copy(item, stage, part).wait()
-                kept = (item % SLOTS, part) + cut(part, stage, place[ORDER[part][stage]])
-                sum_buf[kept] = sum_buf[kept] + rcv[stage][item % SLOTS, part]
+                kept = (lax.rem(item, SLOTS), part) + cut(part, stage, place[ORDER[part][stage]])
+                sum_buf[kept] = sum_buf[kept] + rcv[stage][lax.rem(item, 2), part]
                 rs_copy(item, stage + 1, part).start()
 
     @pl.when(at_lag(1))
@@ -339,7 +309,7 @@
         item = t - 1
         pair_copy(item).wait()
         for part in range(PARTS):
-            sum_buf[item % SLOTS, part] = g_buf[item % SLOTS, part, :, :, :, core] + pair_buf[item % SLOTS, part]
+            sum_buf[lax.rem(item, SLOTS), part] = g_buf[lax.rem(item, 2), part, :, :, :, core] + pair_buf[lax.rem(item, 2), part]
             rs_copy(item, 0, part).start()
 
     @pl.when(t == 0)
@@ -350,6 +320,48 @@
     @pl.when((t >= 1) & (t < n_items))
     def _():
         pair_copy(t).start()
+
+    @pl.when(t == n_items)
+    def _():
+        pack_rows(x_ref, wide, rows, n_img, n_tok)
+
+    @pl.when(t >= first_next)
+    def _():
+        item = n_items - 1 - (t - first_next)
+        rate = sc_ref[0, 1]
+
+        def gathered(part):
+            return all_buf[item, part].reshape(16 * 48, 128).T.astype(F32)
+
+        mixed = gathered(2)
+        nwu_ref[0, :128, :] = wu_ref[0, :128, :] - rate * gathered(0)
+        nwu_ref[0, 128:, :] = wu_ref[0, 128:, :] - rate * mixed[64:, :]
+        nwd_ref[0, :128, :] = wd_ref[0, :128, :] - rate * gathered(1)
+        nwd_ref[0, 128:, :] = wd_ref[0, 128:, :] - rate * mixed[:64, :]
+        up_b = nwu_ref[0].astype(BF16)
+        down_b = nwd_ref[0].astype(BF16)
+        step = rows.shape[0] // CHUNKS
+        for chunk in range(CHUNKS):
+            sl = slice(chunk * step, (chunk + 1) * step)
+            x_wide = rows[sl, :].astype(F32)
+            centered, scale = norm_parts(x_wide)
+            u_rows = (centered * scale).astype(BF16)
+            pre = jnp.dot(u_rows, up_b, preferred_element_type=F32).astype(BF16)
+            z_rows = gelu(pre.astype(F32)).astype(BF16)
+            y_rows = lax.dot_general(z_rows, down_b, LAST, preferred_element_type=F32).astype(BF16)
+            rows[sl, :] = (x_wide + y_rows.astype(F32)).astype(BF16)
+
+    @pl.when(t == pl.num_programs(0) - 1)
+    def _():
+        normed, _ = pooled_norm(rows, n_img, n_tok)
+        norm_ref[...] = normed.astype(BF16)
+        head_ref[...] = all_buf[0]
+
+
+def ticks(n_items):
+    last_update = n_items + 3
+    n_early = (n_items - 3) // 2 + 1
+    return last_update, n_early, n_items - 2 - n_early, last_update + 4
 
 
 def whole(shape):
@@ -410,95 +422,88 @@
 
         head_grad = lax.dot_general(normed, grad_logits, ROWS, preferred_element_type=F32).astype(BF16)
         head_g = head_blocks(head_grad).transpose(1, 0, 2, 3).reshape(PARTS, 2, 2, 2, 2, cols, 128)
+        first_next = ticks(n_items)[3]
+
         def layer_at(t):
+            return jnp.where(t < n_items, jnp.minimum(n_items - 1 - t, n_layers - 1), jnp.maximum(t - first_next, 0))
+
+        def saved_at(t):
             return jnp.clip(n_items - 1 - t, 0, n_layers - 1)
 
         def update_at(t):
             return n_items - 1 - jnp.clip(t - 4, 1, n_items - 1)
 
-        block = (SLOTS, PARTS, 2, 2, 2)
-        mom_head_new, mom_up_new, new_mom_down, gathered = pl.pallas_call(
-            functools.partial(backward_kernel, n_items),
-            grid=(n_items + 9,),
+        def next_at(t):
+            return jnp.maximum(t - first_next, 0)
+
+        block = (PARTS, 2, 2, 2)
+        mom_head_new, mom_up_new, new_mom_down, new_w_up, new_down_t, head_all, normed = pl.pallas_call(
+            functools.partial(update_kernel, n_items, n_img, n_tok),
+            grid=(first_next + n_layers,),
             in_specs=[
                 pl.BlockSpec(memory_space=pltpu.SMEM),
                 whole((PARTS, 2, 2, 2, 2, cols, 128)),
                 whole((n_rows, width)),
-                pl.BlockSpec((1, n_rows, width), lambda t: (layer_at(t), 0, 0)),
-                pl.BlockSpec((1, n_rows, hidden), lambda t: (layer_at(t), 0, 0)),
+                pl.BlockSpec((1, n_rows, width), lambda t: (saved_at(t), 0, 0)),
+                pl.BlockSpec((1, n_rows, hidden), lambda t: (saved_at(t), 0, 0)),
                 pl.BlockSpec((1, width, hidden), lambda t: (layer_at(t), 0, 0)),
                 pl.BlockSpec((1, width, hidden), lambda t: (layer_at(t), 0, 0)),
                 whole((PARTS, cols, 128)),
                 pl.BlockSpec((1, cols, width), lambda t: (update_at(t), 0, 0)),
                 pl.BlockSpec((1, cols, width), lambda t: (update_at(t), 0, 0)),
+                whole((n_img, width, n_tok)),
             ],
             out_specs=[
                 whole((PARTS, cols, 128)),
                 pl.BlockSpec((1, cols, width), lambda t: (update_at(t), 0, 0)),
                 pl.BlockSpec((1, cols, width), lambda t: (update_at(t), 0, 0)),
-                pl.BlockSpec(memory_space=pl.ANY),
+                pl.BlockSpec((1, width, hidden), lambda t: (next_at(t), 0, 0)),
+                pl.BlockSpec((1, width, hidden), lambda t: (next_at(t), 0, 0)),
+                whole((PARTS, 2, 2, 2, 2, cols, 128)),
+                whole((8, width)),
             ],
             out_shape=[
                 jax.ShapeDtypeStruct((PARTS, cols, 128), F32),
                 jax.ShapeDtypeStruct((n_layers, cols, width), F32),
                 jax.ShapeDtypeStruct((n_layers, cols, width), F32),
-                jax.ShapeDtypeStruct((n_items, PARTS, 2, 2, 2, 2, cols, 128), BF16),
+                jax.ShapeDtypeStruct(w_up.shape, F32),
+                jax.ShapeDtypeStruct(w_up.shape, F32),
+                jax.ShapeDtypeStruct((PARTS, 2, 2, 2, 2, cols, 128), BF16),
+                jax.ShapeDtypeStruct((8, width), BF16),
             ],
             scratch_shapes=[
                 pltpu.VMEM((n_rows, width), BF16),
                 pltpu.VMEM((n_rows, hidden), BF16),
                 pltpu.VMEM((n_rows, hidden), BF16),
                 pltpu.VMEM((n_rows, width), BF16),
-                pltpu.VMEM(block + (2, cols, 128), BF16),
-                pltpu.VMEM(block + (cols, 128), BF16),
-                pltpu.VMEM(block + (cols, 128), BF16),
-                pltpu.VMEM((SLOTS, PARTS, 2, 2, cols, 128), BF16),
-                pltpu.VMEM((SLOTS, PARTS, 2, cols, 128), BF16),
-                pltpu.VMEM((SLOTS, PARTS, cols, 128), BF16),
-                pltpu.VMEM((AG_SLOTS, PARTS, 2, 2, 2, 2, cols, 128), BF16),
-                pltpu.SemaphoreType.DMA((2, 2)),
-                pltpu.SemaphoreType.DMA((2, 2)),
+                pltpu.VMEM((n_rows, width), F32),
+                pltpu.VMEM((2,) + block + (2, cols, 128), BF16),
+                pltpu.VMEM((2,) + block + (cols, 128), BF16),
+                pltpu.VMEM((SLOTS,) + block + (cols, 128), BF16),
+                pltpu.VMEM((2, PARTS, 2, 2, cols, 128), BF16),
+                pltpu.VMEM((2, PARTS, 2, cols, 128), BF16),
+                pltpu.VMEM((2, PARTS, cols, 128), BF16),
+                pltpu.VMEM((n_items,) + block + (2, cols, 128), BF16),
+                pltpu.SemaphoreType.DMA((2,)),
+                pltpu.SemaphoreType.DMA((2,)),
+                pltpu.SemaphoreType.DMA((4,)),
+                pltpu.SemaphoreType.DMA((4,)),
                 pltpu.SemaphoreType.DMA((3, PARTS, 2)),
                 pltpu.SemaphoreType.DMA((3, PARTS, 2)),
-                pltpu.SemaphoreType.DMA((3, PARTS, 2)),
-                pltpu.SemaphoreType.DMA((3, PARTS, 2)),
-                pltpu.SemaphoreType.DMA((2,)),
+                pltpu.SemaphoreType.DMA((3, PARTS, 4)),
+                pltpu.SemaphoreType.DMA((3, PARTS, 4)),
             ],
             compiler_params=pltpu.CompilerParams(vmem_limit_bytes=VMEM_LIMIT, collective_id=0, has_side_effects=True),
-            name="step_backward",
-        )(mom_decay.reshape(1, 1), head_g, grad_rows, xs, pre, w_up, down_t, head_blocks(mom_head)[0], mom_up.transpose(0, 2, 1), mom_down)
-
-        gathered = gathered.reshape(n_items, PARTS, n_dev * cols, 128)
-        head_all = gathered[n_layers].reshape(PARTS, n_dev, cols, 128)[:, :, :head_each]
+            name="step_update",
+        )(
+            jnp.stack([mom_decay, learn_rate]).reshape(1, 2), head_g, grad_rows, xs, pre, w_up, down_t,
+            head_blocks(mom_head)[0], mom_up.transpose(0, 2, 1), mom_down, x_next.transpose(0, 2, 1),
+        )
+
+        head_all = head_all.reshape(PARTS, n_dev, cols, 128)[:, :, :head_each]
         head_all = head_all.transpose(1, 0, 2, 3).reshape(n_dev * head_rows, n_tile * 128)[:, :n_cls]
         new_w_head = w_head - learn_rate * head_all.astype(F32)
-
-        new_w_up, new_down_t, logits = pl.pallas_call(
-            functools.partial(next_kernel, n_img, n_tok),
-            grid=(n_layers // per,),
-            in_specs=[
-                pl.BlockSpec(memory_space=pltpu.SMEM),
-                whole((n_img, width, n_tok)),
-                pl.BlockSpec((per, width, hidden), lambda i: (i, 0, 0)),
-                pl.BlockSpec((per, width, hidden), lambda i: (i, 0, 0)),
-                pl.BlockSpec((per, PARTS, n_dev * cols, 128), lambda i: (i, 0, 0, 0)),
-                whole(w_head.shape),
-            ],
-            out_specs=[
-                pl.BlockSpec((per, width, hidden), lambda i: (i, 0, 0)),
-                pl.BlockSpec((per, width, hidden), lambda i: (i, 0, 0)),
-                whole((8, n_cls)),
-            ],
-            out_shape=[
-                jax.ShapeDtypeStruct(w_up.shape, F32),
-                jax.ShapeDtypeStruct(w_up.shape, F32),
-                jax.ShapeDtypeStruct((8, n_cls), F32),
-            ],
-            scratch_shapes=[pltpu.VMEM((n_rows, width), F32), pltpu.VMEM((n_rows, width), BF16)],
-            compiler_params=pltpu.CompilerParams(vmem_limit_bytes=VMEM_LIMIT),
-            name="step_next",
-        )(learn_rate.reshape(1, 1), x_next.transpose(0, 2, 1), w_up, down_t, gathered, new_w_head)
-
+        logits = jnp.dot(normed, new_w_head.astype(BF16), preferred_element_type=F32)
         new_mom_head = mom_head_new[:, :head_each].reshape(head_rows, n_tile * 128)[:, :n_cls]
         return (logits[:n_img], new_w_up, new_down_t.transpose(0, 2, 1), new_w_head, mom_up_new.transpose(0, 2, 1), new_mom_down, new_mom_head)
 

time: 286 us -> 342 us (1.20)
  Pallas kernels: 271 us -> 302 us
  local copies, waits for them, and re-layouts: 10.2 us -> 33.6 us
    pallas_call x2 -> x1, Pallas kernels: 219 us -> 250 us  [local_step(): pl.pallas_call(functools.partial(update_kernel, n_items, n_img, n_tok), g...]
    unnamed x10 -> x22, local copies, waits for them, and re-layouts: 3.81 us -> 27 us
where the time goes in v3:
time: 342 us; the launch traced here: 341 us
  Pallas kernels  302 us (88%)
  local copies, waits for them, and re-layouts  33.6 us (10%)
    pallas_call x1, Pallas kernels, local_step(): pl.pallas_call(functools.partial(update_kernel, n_items, n_img, n_tok), g...  250 us
    pallas_call x1, Pallas kernels, local_step(): pl.pallas_call(functools.partial(forward_kernel, n_img, n_tok, n_img * n_...  52.4 us
    unnamed x22, local copies, waits for them, and re-layouts  27 us

profile of v3, /device:TPU:0, one launch (start us, length us, event | category | flops | bytes accessed | tf_op | source)
XLA Modules:
  0.0 341.2 jit_solution(15533734800705472967)
XLA Ops:
  1.9 0.6 maximum_bitcast_fusion.sc_ref
  2.5 0.7 pad_bitcast_fusion.1
  3.2 0.7 copy.18.lab_ref
  3.9 0.8 pad.23
  4.7 0.6 pad_bitcast_fusion.mh_ref
  5.4 52.4 %step_forward.1 = (bf16[32,800,192]{2,1,0:T(8,128)(2,1)}, bf16[32,800,768]{2,1,0:T(8,128)(2,1)}, bf16[800,192]{1,0:T(8,128)(2,1)}, bf16[8,192]{1,0:T(8,128)(2,1)}, bf16[8,1000]{1,0:T(8,128)(2,1)}) custom-call(bf16[4,192,197]{2,1,0:T(8,128)(2,1)} %bitcast.35, s32[8,1]{1,0:T(8,128)} %copy.18.lab_ref, f32[32,192,768]{2,1,0:T(8,128)} %wu_ref.3, ...), custom_call_target="tpu_custom_call" | custom-call | tf_op jit(solution)/shard_map/step_forward/pallas_call | solution.py:388
  57.8 1.0 convolution_convert_fusion
  58.9 0.2 reshape.40
  59.1 0.9 pad.22
  59.9 0.0 copy-start.1
  59.9 249.8 %step_update.1 = (f32[3,48,128]{2,1,0:T(8,128)}, f32[32,48,192]{2,1,0:T(8,128)}, f32[32,48,192]{2,1,0:T(8,128)}, f32[32,192,768]{2,1,0:T(8,128)}, f32[32,192,768...) custom-call(f32[1,2]{1,0:T(1,128)} %maximum_bitcast_fusion.sc_ref, ...), custom_call_target="tpu_custom_call" | custom-call | tf_op jit(solution)/shard_map/step_update/pallas_call | solution.py:440
  309.7 1.0 slice_bitcast_fusion
  310.8 0.2 reshape.44
  311.0 0.8 slice.18
  311.8 0.6 reshape.45
  312.4 0.0 copy-done.1
  312.4 0.1 multiply_subtract_fusion
  312.5 0.0 copy-start
  312.6 0.0 slice-start
  312.6 1.6 fusion
  314.2 0.0 slice-start.1
  314.2 0.0 slice-start.2
  314.2 0.0 slice-start.3
  314.2 0.0 slice-start.4
  314.2 14.4 %copy.27 = f32[32,192,768]{2,1,0:T(8,128)} copy(f32[32,192,768]{2,1,0:T(8,128)} %get-tuple-element.39) | data formatting | bytes 37748736
  328.6 0.0 copy-done
  328.6 0.0 slice-done
  328.6 0.0 slice-done.1
  328.6 1.0 slice-done.2
  329.6 1.3 slice-done.3
  330.9 0.6 slice-done.4
  331.5 0.0 copy-start.3
  331.5 0.0 copy-start.2
  331.6 7.4 %copy.28 = f32[32,768,192]{1,2,0:T(8,128)} copy(f32[32,768,192]{1,2,0:T(8,128)S(1)} %bitcast.31) | data formatting | bytes 37748736
  338.9 0.0 copy-done.3
  338.9 1.1 copy.29
  340.1 0.0 copy-done.2
  340.1 1.1 copy.30
  (5 shorter events, 0.1 us)
Async XLA Ops:
  59.9 252.5 %copy-start.1 = (f32[192,1000]{1,0:T(8,128)S(1)}, f32[192,1000]{1,0:T(8,128)}, u32[]{:S(2)}) copy-start(f32[192,1000]{1,0:T(8,128)} %wh_ref.1) | copy-start | bytes 2304004
  312.5 16.1 %copy-start = (f32[192,1000]{1,0:T(8,128)}, f32[192,1000]{1,0:T(8,128)S(1)}, u32[]{:S(2)}) copy-start(f32[192,1000]{1,0:T(8,128)S(1)} %multiply_subtract_fusion) | copy-start | bytes 2304004
  312.6 16.0 %slice-start = ((s8[18874368]{0:T(1024)(128)(4,1)}), s8[4194304]{0:T(1024)(128)(4,1)S(1)}, s32[]{:S(2)}) async-start(s8[18874368]{0:T(1024)(128)(4,1)} %bitcast.29), calls=%async_computation | async-start | bytes 8388608
  314.2 14.4 %slice-start.1 = ((s8[18874368]{0:T(1024)(128)(4,1)}), s8[4194304]{0:T(1024)(128)(4,1)S(1)}, s32[]{:S(2)}) async-start(s8[18874368]{0:T(1024)(128)(4,1)} %bitcast.29), calls=%async_computation.1 | async-start | bytes 8388608
  314.2 15.5 %slice-start.2 = ((s8[18874368]{0:T(1024)(128)(4,1)}), s8[4194304]{0:T(1024)(128)(4,1)S(1)}, s32[]{:S(2)}) async-start(s8[18874368]{0:T(1024)(128)(4,1)} %bitcast.29), calls=%async_computation.2 | async-start | bytes 8388608
  314.2 16.8 %slice-start.3 = ((s8[18874368]{0:T(1024)(128)(4,1)}), s8[4194304]{0:T(1024)(128)(4,1)S(1)}, s32[]{:S(2)}) async-start(s8[18874368]{0:T(1024)(128)(4,1)} %bitcast.29), calls=%async_computation.3 | async-start | bytes 8388608
  314.2 17.4 %slice-start.4 = ((s8[18874368]{0:T(1024)(128)(4,1)}), s8[2097152]{0:T(1024)(128)(4,1)S(1)}, s32[]{:S(2)}) async-start(s8[18874368]{0:T(1024)(128)(4,1)} %bitcast.29), calls=%async_computation.4 | async-start | bytes 4194304
  331.5 7.4 %copy-start.3 = (f32[32,48,192]{2,1,0:T(8,128)S(1)}, f32[32,48,192]{2,1,0:T(8,128)}, u32[]{:S(2)}) copy-start(f32[32,48,192]{2,1,0:T(8,128)} %get-tuple-element.28) | copy-start | bytes 3538948
  331.5 8.5 %copy-start.2 = (f32[32,48,192]{2,1,0:T(8,128)S(1)}, f32[32,48,192]{2,1,0:T(8,128)}, u32[]{:S(2)}) copy-start(f32[32,48,192]{2,1,0:T(8,128)} %get-tuple-element.43) | copy-start | bytes 3538948

commit v4 on v2

--- a/solution.py
+++ b/solution.py
@@ -20,6 +20,7 @@
 SLOTS = 4
 AG_SLOTS = 8
 PARTS = 3
+POOL = 16
 ORDER = ((0, 1, 2), (1, 2, 0), (2, 0, 1))
 
 
@@ -65,17 +66,25 @@
 
 def pooled_norm(rows, n_img, n_tok):
     n_rows = rows.shape[0]
-    mask = pool_mask((8, n_rows), n_img, n_tok, 1)
+    mask = pool_mask((POOL, n_rows), n_img, n_tok, 1)
     pooled = jnp.dot(mask, rows[...], preferred_element_type=F32) * (1.0 / n_tok)
     centered, scale = norm_parts(pooled)
     return centered * scale, scale
 
 
-def forward_kernel(n_img, n_tok, batch_total, n_cls, x_ref, lab_ref, wu_ref, wd_ref, wh_ref, xs_ref, pre_ref, grad_ref, norm_ref, gl_ref, wide, rows):
+def forward_kernel(
+    n_img, n_tok, batch_total, head_rows, lab_ref, x_hbm, wu_ref, wd_ref, wh_hbm, xs_ref, pre_ref, grad_hbm, hg_hbm,
+    x_ref, wh_ref, wide, rows, staged, hg_ref, sems,
+):
     layer = pl.program_id(0)
+    x_copy = pltpu.make_async_copy(x_hbm, x_ref, sems.at[0])
+    wh_copy = pltpu.make_async_copy(wh_hbm, wh_ref, sems.at[1])
 
     @pl.when(layer == 0)
     def _():
+        x_copy.start()
+        wh_copy.start()
+        x_copy.wait()
         pack_rows(x_ref, wide, rows, n_img, n_tok)
 
     step = rows.shape[0] // CHUNKS
@@ -97,6 +106,7 @@
 
     @pl.when(layer == pl.num_programs(0) - 1)
     def _():
+        wh_copy.wait()
         normed, scale = pooled_norm(rows, n_img, n_tok)
         normed_b = normed.astype(BF16)
         head_b = wh_ref[...].astype(BF16)
@@ -106,23 +116,47 @@
         probs = exps / jnp.sum(exps, axis=-1, keepdims=True)
         classes = lax.broadcasted_iota(jnp.int32, logits.shape, 1)
         image = lax.broadcasted_iota(jnp.int32, logits.shape, 0)
-        targets = jnp.where(classes == lab_ref[...], 1.0, 0.0)
-        grad_logits = jnp.where(image < n_img, (probs - targets) * (1.0 / batch_total), 0.0)
-        grad_b = grad_logits.astype(BF16)
-        gl_ref[...] = grad_b
-        norm_ref[...] = normed_b
+        hit = jnp.zeros(logits.shape, jnp.bool_)
+        for img in range(n_img):
+            hit = hit | ((image == img) & (classes == lab_ref[img]))
+        targets = jnp.where(hit, 1.0, 0.0)
+        grad_b = jnp.where(image < n_img, (probs - targets) * (1.0 / batch_total), 0.0).astype(BF16)
         grad_normed = lax.dot_general(grad_b, head_b, LAST, preferred_element_type=F32).astype(BF16)
         grad_pooled = norm_pull(normed, scale, grad_normed.astype(F32))
         per_row = (grad_pooled / n_tok).astype(BF16)
-        spread = pool_mask((rows.shape[0], 8), n_img, n_tok, 0)
-        grad_ref[...] = jnp.dot(spread, per_row, preferred_element_type=F32).astype(BF16)
-
-
-def next_kernel(n_img, n_tok, lr_ref, x_ref, wu_ref, wd_ref, mom_ref, wh_ref, nwu_ref, nwd_ref, log_ref, wide, rows):
+        spread = pool_mask((rows.shape[0], POOL), n_img, n_tok, 0)
+        rows[...] = jnp.dot(spread, per_row, preferred_element_type=F32).astype(BF16)
+        grad_copy = pltpu.make_async_copy(rows, grad_hbm, sems.at[0])
+        grad_copy.start()
+        head_grad = lax.dot_general(normed_b, grad_b, ROWS, preferred_element_type=F32).astype(BF16)
+        staged[...] = jnp.zeros_like(staged)
+        staged[: head_grad.shape[0], : head_grad.shape[1]] = head_grad.astype(F32)
+        hg_ref[...] = jnp.zeros_like(hg_ref)
+        for dev in range(16):
+            for tile in range(staged.shape[1] // 128):
+                block = staged[dev * head_rows : dev * head_rows + 16, tile * 128 : (tile + 1) * 128]
+                hg_ref[tile // 3, dev // 8, (dev // 4) % 2, (dev // 2) % 2, dev % 2, (tile % 3) * 16 : (tile % 3) * 16 + 16, :] = block.astype(BF16)
+        hg_copy = pltpu.make_async_copy(hg_ref, hg_hbm, sems.at[1])
+        hg_copy.start()
+        grad_copy.wait()
+        hg_copy.wait()
+
+
+def next_kernel(
+    n_img, n_tok, head_rows, lr_ref, x_hbm, wu_ref, wd_ref, mom_ref, all_hbm, wh_hbm, nwu_ref, nwd_ref, nwh_hbm, log_hbm,
+    x_ref, wh_ref, mh_ref, log_ref, wide, rows, sems,
+):
     layer = pl.program_id(0)
+    x_copy = pltpu.make_async_copy(x_hbm, x_ref, sems.at[0])
+    wh_copy = pltpu.make_async_copy(wh_hbm, wh_ref, sems.at[1])
+    mh_copy = pltpu.make_async_copy(all_hbm.at[all_hbm.shape[0] - 1], mh_ref, sems.at[2])
 
     @pl.when(layer == 0)
     def _():
+        x_copy.start()
+        wh_copy.start()
+        mh_copy.start()
+        x_copy.wait()
         pack_rows(x_ref, wide, rows, n_img, n_tok)
 
     rate = lr_ref[0, 0]
@@ -147,19 +181,35 @@
 
     @pl.when(layer == pl.num_programs(0) - 1)
     def _():
+        wh_copy.wait()
+        mh_copy.wait()
+        n_cls = wh_ref.shape[1]
+        for dev in range(16):
+            for tile in range(-(-n_cls // 128)):
+                span = slice(tile * 128, min(n_cls, (tile + 1) * 128))
+                block = mh_ref[tile // 3, dev * 48 + (tile % 3) * 16 : dev * 48 + (tile % 3) * 16 + 16, :].astype(F32)
+                keep = slice(dev * head_rows, (dev + 1) * head_rows)
+                wh_ref[keep, span] = wh_ref[keep, span] - rate * block[:head_rows, : span.stop - span.start]
+        out_copy = pltpu.make_async_copy(wh_ref, nwh_hbm, sems.at[1])
+        out_copy.start()
         normed, _ = pooled_norm(rows, n_img, n_tok)
-        log_ref[...] = jnp.dot(normed.astype(BF16), wh_ref[...].astype(BF16), preferred_element_type=F32)
+        logits = jnp.dot(normed.astype(BF16), wh_ref[...].astype(BF16), preferred_element_type=F32)
+        log_ref[...] = logits[:n_img]
+        log_copy = pltpu.make_async_copy(log_ref, log_hbm, sems.at[0])
+        log_copy.start()
+        log_copy.wait()
+        out_copy.wait()
 
 
 def backward_kernel(
-    n_items, sc_ref, gh_ref, grad_ref, xs_ref, pre_ref, wu_ref, wd_ref, mh_ref, mu_ref, md_ref, nmh_ref, nmu_ref, nmd_ref, all_ref,
-    g_rows, z_buf, da_buf, u_buf, g_buf, pair_buf, sum_buf, rcv0, rcv1, rcv2, ag_buf,
-    d2d_send, d2d_recv, rs_send, rs_recv, ag_send, ag_recv, out_sem,
+    n_items, sc_ref, gh_hbm, grad_hbm, xs_ref, pre_ref, wu_ref, wd_ref, mh_hbm, mu_hbm, md_hbm, nmh_hbm, nmu_hbm, nmd_hbm, all_ref,
+    g_rows, z_buf, da_buf, u_buf, mh_ref, mu_ref, md_ref, g_buf, pair_buf, sum_buf, rcv0, rcv1, rcv2, ag_buf,
+    d2d_send, d2d_recv, rs_send, rs_recv, ag_send, ag_recv, out_sem, in_sem, mom_sem,
 ):
     t = pl.program_id(0)
     me = lax.axis_index("data")
-    core = me % 2
-    place = ((me // 8) % 2, (me // 4) % 2, (me // 2) % 2)
+    core = lax.rem(me, 2)
+    place = (lax.div(me, 8), lax.rem(lax.div(me, 4), 2), lax.rem(lax.div(me, 2), 2))
     peers = tuple(me + (1 - 2 * place[axis]) * w for axis, w in ((0, 8), (1, 4), (2, 2)))
     twin = me + 1 - 2 * core
     rcv = (rcv0, rcv1, rcv2)
@@ -173,10 +223,10 @@
 
     def pair_copy(item):
         return pltpu.make_async_remote_copy(
-            src_ref=g_buf.at[item % SLOTS, :, :, :, :, 1 - core],
-            dst_ref=pair_buf.at[item % SLOTS],
-            send_sem=d2d_send.at[0, item % 2],
-            recv_sem=d2d_recv.at[0, item % 2],
+            src_ref=g_buf.at[lax.rem(item, SLOTS), :, :, :, :, 1 - core],
+            dst_ref=pair_buf.at[lax.rem(item, SLOTS)],
+            send_sem=d2d_send.at[0, lax.rem(item, 2)],
+            recv_sem=d2d_recv.at[0, lax.rem(item, 2)],
             device_id=(twin,),
             device_id_type=MESH_ID,
         )
@@ -191,10 +241,10 @@
     def rs_copy(item, stage, part):
         axis = ORDER[part][stage]
         return pltpu.make_async_remote_copy(
-            src_ref=sum_buf.at[(item % SLOTS, part) + cut(part, stage, 1 - place[axis])],
-            dst_ref=rcv[stage].at[item % SLOTS, part],
-            send_sem=rs_send.at[stage, part, item % 2],
-            recv_sem=rs_recv.at[stage, part, item % 2],
+            src_ref=sum_buf.at[(lax.rem(item, SLOTS), part) + cut(part, stage, 1 - place[axis])],
+            dst_ref=rcv[stage].at[lax.rem(item, SLOTS), part],
+            send_sem=rs_send.at[stage, part, lax.rem(item, 2)],
+            recv_sem=rs_recv.at[stage, part, lax.rem(item, 2)],
             device_id=(peers[axis],),
             device_id_type=MESH_ID,
         )
@@ -203,36 +253,52 @@
         index = [place[0], place[1], place[2]]
         for axis in ORDER[part][:stage]:
             index[axis] = slice(None)
-        view = ag_buf.at[(item % AG_SLOTS, part) + tuple(index) + (core,)]
+        view = ag_buf.at[(lax.rem(item, AG_SLOTS), part) + tuple(index) + (core,)]
         return pltpu.make_async_remote_copy(
             src_ref=view,
             dst_ref=view,
-            send_sem=ag_send.at[stage, part, item % 2],
-            recv_sem=ag_recv.at[stage, part, item % 2],
+            send_sem=ag_send.at[stage, part, lax.rem(item, 2)],
+            recv_sem=ag_recv.at[stage, part, lax.rem(item, 2)],
             device_id=(peers[ORDER[part][stage]],),
             device_id_type=MESH_ID,
         )
 
     def twin_copy(item):
-        view = ag_buf.at[item % AG_SLOTS, :, :, :, :, core]
+        view = ag_buf.at[lax.rem(item, AG_SLOTS), :, :, :, :, core]
         return pltpu.make_async_remote_copy(
             src_ref=view,
             dst_ref=view,
-            send_sem=d2d_send.at[1, item % 2],
-            recv_sem=d2d_recv.at[1, item % 2],
+            send_sem=d2d_send.at[1, lax.rem(item, 2)],
+            recv_sem=d2d_recv.at[1, lax.rem(item, 2)],
             device_id=(twin,),
             device_id_type=MESH_ID,
         )
 
     def out_copy(item):
-        return pltpu.make_async_copy(ag_buf.at[item % AG_SLOTS], all_ref.at[n_items - 1 - item], out_sem.at[item % 2])
+        return pltpu.make_async_copy(ag_buf.at[lax.rem(item, AG_SLOTS)], all_ref.at[n_items - 1 - item], out_sem.at[lax.rem(item, 2)])
 
     def at_lag(lag):
         return (t >= lag) & (t < n_items + lag)
 
+    head_copy = pltpu.make_async_copy(gh_hbm, g_buf.at[0], in_sem.at[0])
+    grad_copy = pltpu.make_async_copy(grad_hbm, g_rows, in_sem.at[1])
+    moms = tuple(
+        pltpu.make_async_copy(src, dst, in_sem.at[2 + i]) for i, (src, dst) in enumerate(((mh_hbm, mh_ref), (mu_hbm, mu_ref), (md_hbm, md_ref)))
+    )
+    moms_out = tuple(
+        pltpu.make_async_copy(src, dst, mom_sem.at[i]) for i, (src, dst) in enumerate(((mh_ref, nmh_hbm), (mu_ref, nmu_hbm), (md_ref, nmd_hbm)))
+    )
+
+    @pl.when(t == 0)
+    def _():
+        head_copy.start()
+        grad_copy.start()
+        for copy in moms:
+            copy.start()
+
     @pl.when(t == 1)
     def _():
-        g_rows[...] = grad_ref[...]
+        grad_copy.wait()
 
     @pl.when((t >= 1) & (t < n_items))
     def _():
@@ -260,7 +326,7 @@
             turned = value.T
             for dev in range(16):
                 block = turned[dev * 48 : (dev + 1) * 48, :]
-                g_buf[t % SLOTS, part, dev // 8, (dev // 4) % 2, (dev // 2) % 2, dev % 2] = block
+                g_buf[lax.rem(t, SLOTS), part, dev // 8, (dev // 4) % 2, (dev // 2) % 2, dev % 2] = block
 
     @pl.when(at_lag(9))
     def _():
@@ -295,30 +361,33 @@
             rs_copy(item, 2, part).wait()
 
         def reduced(part):
-            return (sum_buf[item % SLOTS, part, place[0], place[1], place[2]] + rcv[2][item % SLOTS, part]).astype(F32)
+            return (sum_buf[lax.rem(item, SLOTS), part, place[0], place[1], place[2]] + rcv[2][lax.rem(item, SLOTS), part]).astype(F32)
 
         def hand_on(part, mom):
-            ag_buf[item % AG_SLOTS, part, place[0], place[1], place[2], core] = mom.astype(BF16)
+            ag_buf[lax.rem(item, AG_SLOTS), part, place[0], place[1], place[2], core] = mom.astype(BF16)
             ag_copy(item, 0, part).start()
 
         @pl.when(t == 4)
         def _():
+            for copy in moms:
+                copy.wait()
             for part in range(PARTS):
                 mom = sc_ref[0, 0] * mh_ref[part] + reduced(part)
-                nmh_ref[part] = mom
+                mh_ref[part] = mom
                 hand_on(part, mom)
 
         @pl.when(t > 4)
         def _():
+            layer = n_items - 1 - item
             mixed = reduced(2)
-            up_a = sc_ref[0, 0] * mu_ref[0, :, :128] + reduced(0)
-            down_a = sc_ref[0, 0] * md_ref[0, :, :128] + reduced(1)
-            up_z = sc_ref[0, 0] * mu_ref[0, :, 128:] + mixed[:, 64:]
-            down_z = sc_ref[0, 0] * md_ref[0, :, 128:] + mixed[:, :64]
-            nmu_ref[0, :, :128] = up_a
-            nmu_ref[0, :, 128:] = up_z
-            nmd_ref[0, :, :128] = down_a
-            nmd_ref[0, :, 128:] = down_z
+            up_a = sc_ref[0, 0] * mu_ref[layer, :, :128] + reduced(0)
+            down_a = sc_ref[0, 0] * md_ref[layer, :, :128] + reduced(1)
+            up_z = sc_ref[0, 0] * mu_ref[layer, :, 128:] + mixed[:, 64:]
+            down_z = sc_ref[0, 0] * md_ref[layer, :, 128:] + mixed[:, :64]
+            mu_ref[layer, :, :128] = up_a
+            mu_ref[layer, :, 128:] = up_z
+            md_ref[layer, :, :128] = down_a
+            md_ref[layer, :, 128:] = down_z
             hand_on(0, up_a)
             hand_on(1, down_a)
             hand_on(2, jnp.concatenate([down_z, up_z], axis=1))
@@ -330,8 +399,8 @@
             item = t - 2 - stage
             for part in range(PARTS):
                 rs_copy(item, stage, part).wait()
-                kept = (item % SLOTS, part) + cut(part, stage, place[ORDER[part][stage]])
-                sum_buf[kept] = sum_buf[kept] + rcv[stage][item % SLOTS, part]
+                kept = (lax.rem(item, SLOTS), part) + cut(part, stage, place[ORDER[part][stage]])
+                sum_buf[kept] = sum_buf[kept] + rcv[stage][lax.rem(item, SLOTS), part]
                 rs_copy(item, stage + 1, part).start()
 
     @pl.when(at_lag(1))
@@ -339,21 +408,27 @@
         item = t - 1
         pair_copy(item).wait()
         for part in range(PARTS):
-            sum_buf[item % SLOTS, part] = g_buf[item % SLOTS, part, :, :, :, core] + pair_buf[item % SLOTS, part]
+            sum_buf[lax.rem(item, SLOTS), part] = g_buf[lax.rem(item, SLOTS), part, :, :, :, core] + pair_buf[lax.rem(item, SLOTS), part]
             rs_copy(item, 0, part).start()
 
     @pl.when(t == 0)
     def _():
-        g_buf[0] = gh_ref[...]
+        head_copy.wait()
         pair_copy(0).start()
 
     @pl.when((t >= 1) & (t < n_items))
     def _():
         pair_copy(t).start()
 
-
-def whole(shape):
-    return pl.BlockSpec(shape, lambda i: (0,) * len(shape))
+    @pl.when(t == n_items + 4)
+    def _():
+        for copy in moms_out:
+            copy.start()
+
+    @pl.when(t == n_items + 6)
+    def _():
+        for copy in moms_out:
+            copy.wait()
 
 
 def solution(mesh):
@@ -368,53 +443,51 @@
         cols = mom_up.shape[2]
         head_rows = mom_head.shape[0]
         n_tile = -(-n_cls // 128)
-        head_each = head_rows * n_tile // PARTS
 
         down_t = w_down.transpose(0, 2, 1)
         per = 2 if n_layers % 2 == 0 else 1
-        lab = jnp.pad(labels, (0, 8 - n_img)).reshape(8, 1)
-        xs, pre, grad_rows, normed, grad_logits = pl.pallas_call(
-            functools.partial(forward_kernel, n_img, n_tok, n_img * n_dev, n_cls),
+        any_spec = pl.BlockSpec(memory_space=pl.ANY)
+        blocks = (PARTS, 2, 2, 2, 2, cols, 128)
+        xs, pre, grad_rows, head_g = pl.pallas_call(
+            functools.partial(forward_kernel, n_img, n_tok, n_img * n_dev, head_rows),
             grid=(n_layers // per,),
             in_specs=[
-                whole((n_img, width, n_tok)),
-                whole((8, 1)),
+                pl.BlockSpec(memory_space=pltpu.SMEM),
+                any_spec,
                 pl.BlockSpec((per, width, hidden), lambda i: (i, 0, 0)),
                 pl.BlockSpec((per, width, hidden), lambda i: (i, 0, 0)),
-                whole(w_head.shape),
+                any_spec,
             ],
             out_specs=[
                 pl.BlockSpec((per, n_rows, width), lambda i: (i, 0, 0)),
                 pl.BlockSpec((per, n_rows, hidden), lambda i: (i, 0, 0)),
-                whole((n_rows, width)),
-                whole((8, width)),
-                whole((8, n_cls)),
+                any_spec,
+                any_spec,
             ],
             out_shape=[
                 jax.ShapeDtypeStruct((n_layers, n_rows, width), BF16),
                 jax.ShapeDtypeStruct((n_layers, n_rows, hidden), BF16),
                 jax.ShapeDtypeStruct((n_rows, width), BF16),
-                jax.ShapeDtypeStruct((8, width), BF16),
-                jax.ShapeDtypeStruct((8, n_cls), BF16),
-            ],
-            scratch_shapes=[pltpu.VMEM((n_rows, width), F32), pltpu.VMEM((n_rows, width), BF16)],
+                jax.ShapeDtypeStruct(blocks, BF16),
+            ],
+            scratch_shapes=[
+                pltpu.VMEM((n_img, width, n_tok), BF16),
+                pltpu.VMEM(w_head.shape, F32),
+                pltpu.VMEM((n_rows, width), F32),
+                pltpu.VMEM((n_rows, width), BF16),
+                pltpu.VMEM((n_dev * head_rows + 16, n_tile * 128), F32),
+                pltpu.VMEM(blocks, BF16),
+                pltpu.SemaphoreType.DMA((2,)),
+            ],
             compiler_params=pltpu.CompilerParams(vmem_limit_bytes=VMEM_LIMIT),
             name="step_forward",
-        )(x_now.transpose(0, 2, 1), lab, w_up, down_t, w_head)
-
-        def head_blocks(values):
-            n_part = values.shape[0] // head_rows
-            wide = jnp.pad(values, ((0, 0), (0, n_tile * 128 - n_cls)))
-            blocks = wide.reshape(n_part, PARTS, head_each, 128)
-            return jnp.pad(blocks, ((0, 0), (0, 0), (0, cols - head_each), (0, 0)))
-
-        head_grad = lax.dot_general(normed, grad_logits, ROWS, preferred_element_type=F32).astype(BF16)
-        head_g = head_blocks(head_grad).transpose(1, 0, 2, 3).reshape(PARTS, 2, 2, 2, 2, cols, 128)
+        )(labels, x_now.transpose(0, 2, 1), w_up, down_t, w_head)
+
+        head_m = jnp.pad(mom_head, ((0, 16 - head_rows), (0, 9 * 128 - n_cls))).reshape(16, 9, 128)
+        head_m = head_m.transpose(1, 0, 2).reshape(PARTS, cols, 128)
+
         def layer_at(t):
             return jnp.clip(n_items - 1 - t, 0, n_layers - 1)
-
-        def update_at(t):
-            return n_items - 1 - jnp.clip(t - 4, 1, n_items - 1)
 
         block = (SLOTS, PARTS, 2, 2, 2)
         mom_head_new, mom_up_new, new_mom_down, gathered = pl.pallas_call(
@@ -422,22 +495,17 @@
             grid=(n_items + 9,),
             in_specs=[
                 pl.BlockSpec(memory_space=pltpu.SMEM),
-                whole((PARTS, 2, 2, 2, 2, cols, 128)),
-                whole((n_rows, width)),
+                any_spec,
+                any_spec,
                 pl.BlockSpec((1, n_rows, width), lambda t: (layer_at(t), 0, 0)),
                 pl.BlockSpec((1, n_rows, hidden), lambda t: (layer_at(t), 0, 0)),
                 pl.BlockSpec((1, width, hidden), lambda t: (layer_at(t), 0, 0)),
                 pl.BlockSpec((1, width, hidden), lambda t: (layer_at(t), 0, 0)),
-                whole((PARTS, cols, 128)),
-                pl.BlockSpec((1, cols, width), lambda t: (update_at(t), 0, 0)),
-                pl.BlockSpec((1, cols, width), lambda t: (update_at(t), 0, 0)),
-            ],
-            out_specs=[
-                whole((PARTS, cols, 128)),
-                pl.BlockSpec((1, cols, width), lambda t: (update_at(t), 0, 0)),
-                pl.BlockSpec((1, cols, width), lambda t: (update_at(t), 0, 0)),
-                pl.BlockSpec(memory_space=pl.ANY),
-            ],
+                any_spec,
+                any_spec,
+                any_spec,
+            ],
+            out_specs=[any_spec] * 4,
             out_shape=[
                 jax.ShapeDtypeStruct((PARTS, cols, 128), F32),
                 jax.ShapeDtypeStruct((n_layers, cols, width), F32),
@@ -449,6 +517,9 @@
                 pltpu.VMEM((n_rows, hidden), BF16),
                 pltpu.VMEM((n_rows, hidden), BF16),
                 pltpu.VMEM((n_rows, width), BF16),
+                pltpu.VMEM((PARTS, cols, 128), F32),
+                pltpu.VMEM((n_layers, cols, width), F32),
+                pltpu.VMEM((n_layers, cols, width), F32),
                 pltpu.VMEM(block + (2, cols, 128), BF16),
                 pltpu.VMEM(block + (cols, 128), BF16),
                 pltpu.VMEM(block + (cols, 128), BF16),
@@ -463,44 +534,53 @@
                 pltpu.SemaphoreType.DMA((3, PARTS, 2)),
                 pltpu.SemaphoreType.DMA((3, PARTS, 2)),
                 pltpu.SemaphoreType.DMA((2,)),
+                pltpu.SemaphoreType.DMA((5,)),
+                pltpu.SemaphoreType.DMA((3,)),
             ],
             compiler_params=pltpu.CompilerParams(vmem_limit_bytes=VMEM_LIMIT, collective_id=0, has_side_effects=True),
             name="step_backward",
-        )(mom_decay.reshape(1, 1), head_g, grad_rows, xs, pre, w_up, down_t, head_blocks(mom_head)[0], mom_up.transpose(0, 2, 1), mom_down)
+        )(mom_decay.reshape(1, 1), head_g, grad_rows, xs, pre, w_up, down_t, head_m, mom_up.transpose(0, 2, 1), mom_down)
 
         gathered = gathered.reshape(n_items, PARTS, n_dev * cols, 128)
-        head_all = gathered[n_layers].reshape(PARTS, n_dev, cols, 128)[:, :, :head_each]
-        head_all = head_all.transpose(1, 0, 2, 3).reshape(n_dev * head_rows, n_tile * 128)[:, :n_cls]
-        new_w_head = w_head - learn_rate * head_all.astype(F32)
-
-        new_w_up, new_down_t, logits = pl.pallas_call(
-            functools.partial(next_kernel, n_img, n_tok),
+        new_w_up, new_down_t, new_w_head, logits = pl.pallas_call(
+            functools.partial(next_kernel, n_img, n_tok, head_rows),
             grid=(n_layers // per,),
             in_specs=[
                 pl.BlockSpec(memory_space=pltpu.SMEM),
-                whole((n_img, width, n_tok)),
+                any_spec,
                 pl.BlockSpec((per, width, hidden), lambda i: (i, 0, 0)),
                 pl.BlockSpec((per, width, hidden), lambda i: (i, 0, 0)),
                 pl.BlockSpec((per, PARTS, n_dev * cols, 128), lambda i: (i, 0, 0, 0)),
-                whole(w_head.shape),
+                any_spec,
+                any_spec,
             ],
             out_specs=[
                 pl.BlockSpec((per, width, hidden), lambda i: (i, 0, 0)),
                 pl.BlockSpec((per, width, hidden), lambda i: (i, 0, 0)),
-                whole((8, n_cls)),
+                any_spec,
+                any_spec,
             ],
             out_shape=[
                 jax.ShapeDtypeStruct(w_up.shape, F32),
                 jax.ShapeDtypeStruct(w_up.shape, F32),
-                jax.ShapeDtypeStruct((8, n_cls), F32),
-            ],
-            scratch_shapes=[pltpu.VMEM((n_rows, width), F32), pltpu.VMEM((n_rows, width), BF16)],
+                jax.ShapeDtypeStruct(w_head.shape, F32),
+                jax.ShapeDtypeStruct((n_img, n_cls), F32),
+            ],
+            scratch_shapes=[
+                pltpu.VMEM((n_img, width, n_tok), BF16),
+                pltpu.VMEM(w_head.shape, F32),
+                pltpu.VMEM((PARTS, n_dev * cols, 128), BF16),
+                pltpu.VMEM((n_img, n_cls), F32),
+                pltpu.VMEM((n_rows, width), F32),
+                pltpu.VMEM((n_rows, width), BF16),
+                pltpu.SemaphoreType.DMA((3,)),
+            ],
             compiler_params=pltpu.CompilerParams(vmem_limit_bytes=VMEM_LIMIT),
             name="step_next",
-        )(learn_rate.reshape(1, 1), x_next.transpose(0, 2, 1), w_up, down_t, gathered, new_w_head)
-
-        new_mom_head = mom_head_new[:, :head_each].reshape(head_rows, n_tile * 128)[:, :n_cls]
-        return (logits[:n_img], new_w_up, new_down_t.transpose(0, 2, 1), new_w_head, mom_up_new.transpose(0, 2, 1), new_mom_down, new_mom_head)
+        )(learn_rate.reshape(1, 1), x_next.transpose(0, 2, 1), w_up, down_t, gathered, gathered, w_head)
+
+        new_mom_head = mom_head_new.reshape(9, 16, 128).transpose(1, 0, 2).reshape(16, 9 * 128)[:head_rows, :n_cls]
+        return (logits, new_w_up, new_down_t.transpose(0, 2, 1), new_w_head, mom_up_new.transpose(0, 2, 1), new_mom_down, new_mom_head)
 
     spec_up = P(None, None, "data")
     spec_down = P(None, "data", None)

time: 286 us -> 283 us (0.990)
  local copies, waits for them, and re-layouts: 10.2 us -> 5.19 us
  Pallas kernels: 271 us -> 275 us
where the time goes in v4:
time: 283 us; the launch traced here: 282 us
  Pallas kernels  275 us (97%)
  local copies, waits for them, and re-layouts  5.19 us (2%)
    pallas_call x1, Pallas kernels, local_step(): pl.pallas_call(functools.partial(backward_kernel, n_items), grid=(n_items...  163 us
    pallas_call x1, Pallas kernels, local_step(): pl.pallas_call(functools.partial(next_kernel, n_img, n_tok, head_rows), g...  58.1 us
    pallas_call x1, Pallas kernels, local_step(): pl.pallas_call(functools.partial(forward_kernel, n_img, n_tok, n_img * n_...  54.1 us

profile of v4, /device:TPU:0, one launch (start us, length us, event | category | flops | bytes accessed | tf_op | source)
XLA Modules:
  0.0 282.4 jit_solution(5340718731585372173)
XLA Ops:
  0.6 0.0 copy-start.2
  0.6 54.1 %step_forward.1 = (bf16[32,800,192]{2,1,0:T(8,128)(2,1)}, bf16[32,800,768]{2,1,0:T(8,128)(2,1)}, bf16[800,192]{1,0:T(8,128)(2,1)}, bf16[3,2,2,2,2,48,128]{6,5,4,3,2,1,0:T(8,128)(2,1)}) custom-call(s32[4]{0:T(128)} %lab_ref.1, bf16[4,192,197]{2,1,0:T(8,128)(2,1)} %bitcast.28, f32[32,192,768]{2,1,0:T(8,128)} %wu_ref.5, f32[32,192,768]{2,1,0:T(8,128)} %bitcast.19, ...), custom_call_target="tpu_custom_call" | custom-call | tf_op jit(solution)/shard_map/step_forward/pallas_call | solution.py:451
  54.7 0.0 copy-done.2
  54.8 0.7 copy.20
  56.1 163.0 %step_backward.1 = (f32[3,48,128]{2,1,0:T(8,128)}, f32[32,48,192]{2,1,0:T(8,128)}, f32[32,48,192]{2,1,0:T(8,128)}, bf16[33,3,2,2,2,2,48,128]{7,6,5,4,3,2,1,0:T(8,128)(2,1)}) custom-call(f32[1,1]{1,0:T(1,128)} %bitcast.18.sc_ref, bf16[3,2,2,2,2,48,128]{6,5,4,3,2,1,0:T(8,128)(2,1)} %get-tuple-element.19.gh_hbm, bf16[800,192]{1,0:T(8,128)(2,1)} %get-tuple-element.20.grad_hbm, ...), custom_call_target="tpu_custom_call" | custom-call | tf_op jit(solution)/shard_map/step_backward/pallas_call | solution.py:493
  219.7 0.0 copy-start.1
  219.7 0.0 copy-start
  219.7 58.1 %step_next.1 = (f32[32,192,768]{2,1,0:T(8,128)}, f32[32,192,768]{2,1,0:T(8,128)}, f32[192,1000]{1,0:T(8,128)}, f32[4,1000]{1,0:T(4,128)}) custom-call(f32[1,1]{1,0:T(1,128)} %bitcast.17.lr_ref, bf16[4,192,197]{2,1,0:T(8,128)(2,1)} %bitcast.29, f32[32,192,768]{2,1,0:T(8,128)} %wu_ref.5, f32[32,192,768]{2,1,0:T(8,128)} %bitcast.21, ...), custom_call_target="tpu_custom_call" | custom-call | tf_op jit(solution)/shard_map/step_next/pallas_call | solution.py:545
  277.8 0.0 copy-done.1
  277.9 0.6 slice.4
  278.6 2.7 copy.29
  281.2 0.0 copy-done
  281.2 1.1 copy.30
  (4 shorter events, 0.1 us)
Async XLA Ops:
  0.6 54.1 %copy-start.2 = (f32[12,1000]{1,0:T(8,128)S(1)}, f32[12,1000]{1,0:T(8,128)}, u32[]{:S(2)}) copy-start(f32[12,1000]{1,0:T(8,128)} %param.19) | copy-start | bytes 144004
  219.7 58.2 %copy-start.1 = (f32[3,48,128]{2,1,0:T(8,128)S(1)}, f32[3,48,128]{2,1,0:T(8,128)}, u32[]{:S(2)}) copy-start(f32[3,48,128]{2,1,0:T(8,128)} %get-tuple-element.30) | copy-start | bytes 221188
  219.7 61.5 %copy-start = (f32[32,48,192]{2,1,0:T(8,128)S(1)}, f32[32,48,192]{2,1,0:T(8,128)}, u32[]{:S(2)}) copy-start(f32[32,48,192]{2,1,0:T(8,128)} %get-tuple-element.43) | copy-start | bytes 3538948

commit v5 on v4

--- a/solution.py
+++ b/solution.py
@@ -17,8 +17,12 @@
 MESH_ID = pl.DeviceIdType.MESH
 VMEM_LIMIT = 62 * 1024 * 1024
 CHUNKS = 5
-SLOTS = 4
-AG_SLOTS = 8
+G_SLOTS = 2
+RS_SLOTS = 8
+IN_SLOTS = 4
+AG_SLOTS = 12
+UPDATE = 7
+TWIN = 13
 PARTS = 3
 POOL = 16
 ORDER = ((0, 1, 2), (1, 2, 0), (2, 0, 1))
@@ -222,11 +226,12 @@
         pl.semaphore_wait(barrier, 4)
 
     def pair_copy(item):
+        slot = lax.rem(item, G_SLOTS)
         return pltpu.make_async_remote_copy(
-            src_ref=g_buf.at[lax.rem(item, SLOTS), :, :, :, :, 1 - core],
-            dst_ref=pair_buf.at[lax.rem(item, SLOTS)],
-            send_sem=d2d_send.at[0, lax.rem(item, 2)],
-            recv_sem=d2d_recv.at[0, lax.rem(item, 2)],
+            src_ref=g_buf.at[slot, :, :, :, :, 1 - core],
+            dst_ref=pair_buf.at[slot],
+            send_sem=d2d_send.at[0, slot],
+            recv_sem=d2d_recv.at[0, slot],
             device_id=(twin,),
             device_id_type=MESH_ID,
         )
@@ -240,11 +245,12 @@
 
     def rs_copy(item, stage, part):
         axis = ORDER[part][stage]
+        slot = lax.rem(item, IN_SLOTS)
         return pltpu.make_async_remote_copy(
-            src_ref=sum_buf.at[(lax.rem(item, SLOTS), part) + cut(part, stage, 1 - place[axis])],
-            dst_ref=rcv[stage].at[lax.rem(item, SLOTS), part],
-            send_sem=rs_send.at[stage, part, lax.rem(item, 2)],
-            recv_sem=rs_recv.at[stage, part, lax.rem(item, 2)],
+            src_ref=sum_buf.at[(lax.rem(item, RS_SLOTS), part) + cut(part, stage, 1 - place[axis])],
+            dst_ref=rcv[stage].at[slot, part],
+            send_sem=rs_send.at[stage, part, slot],
+            recv_sem=rs_recv.at[stage, part, slot],
             device_id=(peers[axis],),
             device_id_type=MESH_ID,
         )
@@ -257,8 +263,8 @@
         return pltpu.make_async_remote_copy(
             src_ref=view,
             dst_ref=view,
-            send_sem=ag_send.at[stage, part, lax.rem(item, 2)],
-            recv_sem=ag_recv.at[stage, part, lax.rem(item, 2)],
+            send_sem=ag_send.at[stage, part, lax.rem(item, IN_SLOTS)],
+            recv_sem=ag_recv.at[stage, part, lax.rem(item, IN_SLOTS)],
             device_id=(peers[ORDER[part][stage]],),
             device_id_type=MESH_ID,
         )
@@ -326,48 +332,21 @@
             turned = value.T
             for dev in range(16):
                 block = turned[dev * 48 : (dev + 1) * 48, :]
-                g_buf[lax.rem(t, SLOTS), part, dev // 8, (dev // 4) % 2, (dev // 2) % 2, dev % 2] = block
-
-    @pl.when(at_lag(9))
-    def _():
-        out_copy(t - 9).wait()
-
-    @pl.when(at_lag(8))
-    def _():
-        item = t - 8
-        twin_copy(item).wait()
-        out_copy(item).start()
-
-    @pl.when(at_lag(7))
-    def _():
-        item = t - 7
-        for part in range(PARTS):
-            ag_copy(item, 2, part).wait()
-        twin_copy(item).start()
-
-    for stage in (1, 0):
-
-        @pl.when(at_lag(5 + stage))
-        def _(stage=stage):
-            item = t - 5 - stage
-            for part in range(PARTS):
-                ag_copy(item, stage, part).wait()
-                ag_copy(item, stage + 1, part).start()
-
-    @pl.when(at_lag(4))
-    def _():
-        item = t - 4
+                g_buf[lax.rem(t, G_SLOTS), part, dev // 8, (dev // 4) % 2, (dev // 2) % 2, dev % 2] = block
+
+    @pl.when(at_lag(UPDATE))
+    def _():
+        item = t - UPDATE
         for part in range(PARTS):
             rs_copy(item, 2, part).wait()
 
         def reduced(part):
-            return (sum_buf[lax.rem(item, SLOTS), part, place[0], place[1], place[2]] + rcv[2][lax.rem(item, SLOTS), part]).astype(F32)
+            return (sum_buf[lax.rem(item, RS_SLOTS), part, place[0], place[1], place[2]] + rcv[2][lax.rem(item, IN_SLOTS), part]).astype(F32)
 
         def hand_on(part, mom):
             ag_buf[lax.rem(item, AG_SLOTS), part, place[0], place[1], place[2], core] = mom.astype(BF16)
-            ag_copy(item, 0, part).start()
-
-        @pl.when(t == 4)
+
+        @pl.when(t == UPDATE)
         def _():
             for copy in moms:
                 copy.wait()
@@ -376,7 +355,7 @@
                 mh_ref[part] = mom
                 hand_on(part, mom)
 
-        @pl.when(t > 4)
+        @pl.when(t > UPDATE)
         def _():
             layer = n_items - 1 - item
             mixed = reduced(2)
@@ -394,13 +373,13 @@
 
     for stage in (1, 0):
 
-        @pl.when(at_lag(2 + stage))
+        @pl.when(at_lag(3 + 2 * stage))
         def _(stage=stage):
-            item = t - 2 - stage
+            item = t - 3 - 2 * stage
             for part in range(PARTS):
                 rs_copy(item, stage, part).wait()
-                kept = (lax.rem(item, SLOTS), part) + cut(part, stage, place[ORDER[part][stage]])
-                sum_buf[kept] = sum_buf[kept] + rcv[stage][lax.rem(item, SLOTS), part]
+                kept = (lax.rem(item, RS_SLOTS), part) + cut(part, stage, place[ORDER[part][stage]])
+                sum_buf[kept] = sum_buf[kept] + rcv[stage][lax.rem(item, IN_SLOTS), part]
                 rs_copy(item, stage + 1, part).start()
 
     @pl.when(at_lag(1))
@@ -408,7 +387,8 @@
         item = t - 1
         pair_copy(item).wait()
         for part in range(PARTS):
-            sum_buf[lax.rem(item, SLOTS), part] = g_buf[lax.rem(item, SLOTS), part, :, :, :, core] + pair_buf[lax.rem(item, SLOTS), part]
+            kept = g_buf[lax.rem(item, G_SLOTS), part, :, :, :, core]
+            sum_buf[lax.rem(item, RS_SLOTS), part] = kept + pair_buf[lax.rem(item, G_SLOTS), part]
             rs_copy(item, 0, part).start()
 
     @pl.when(t == 0)
@@ -420,12 +400,39 @@
     def _():
         pair_copy(t).start()
 
-    @pl.when(t == n_items + 4)
+    @pl.when(at_lag(TWIN + 2))
+    def _():
+        out_copy(t - TWIN - 2).wait()
+
+    @pl.when(at_lag(TWIN + 1))
+    def _():
+        item = t - TWIN - 1
+        twin_copy(item).wait()
+        out_copy(item).start()
+
+    for stage in (3, 2, 1):
+
+        @pl.when(at_lag(UPDATE + 2 * stage))
+        def _(stage=stage):
+            item = t - UPDATE - 2 * stage
+            for part in range(PARTS):
+                ag_copy(item, stage - 1, part).wait()
+                if stage < 3:
+                    ag_copy(item, stage, part).start()
+            if stage == 3:
+                twin_copy(item).start()
+
+    @pl.when(at_lag(UPDATE))
+    def _():
+        for part in range(PARTS):
+            ag_copy(t - UPDATE, 0, part).start()
+
+    @pl.when(t == n_items + UPDATE)
     def _():
         for copy in moms_out:
             copy.start()
 
-    @pl.when(t == n_items + 6)
+    @pl.when(t == n_items + UPDATE + 3)
     def _():
         for copy in moms_out:
             copy.wait()
@@ -489,10 +496,10 @@
         def layer_at(t):
             return jnp.clip(n_items - 1 - t, 0, n_layers - 1)
 
-        block = (SLOTS, PARTS, 2, 2, 2)
+        block = (PARTS, 2, 2, 2)
         mom_head_new, mom_up_new, new_mom_down, gathered = pl.pallas_call(
             functools.partial(backward_kernel, n_items),
-            grid=(n_items + 9,),
+            grid=(n_items + TWIN + 2,),
             in_specs=[
                 pl.BlockSpec(memory_space=pltpu.SMEM),
                 any_spec,
@@ -520,19 +527,19 @@
                 pltpu.VMEM((PARTS, cols, 128), F32),
                 pltpu.VMEM((n_layers, cols, width), F32),
                 pltpu.VMEM((n_layers, cols, width), F32),
-                pltpu.VMEM(block + (2, cols, 128), BF16),
-                pltpu.VMEM(block + (cols, 128), BF16),
-                pltpu.VMEM(block + (cols, 128), BF16),
-                pltpu.VMEM((SLOTS, PARTS, 2, 2, cols, 128), BF16),
-                pltpu.VMEM((SLOTS, PARTS, 2, cols, 128), BF16),
-                pltpu.VMEM((SLOTS, PARTS, cols, 128), BF16),
-                pltpu.VMEM((AG_SLOTS, PARTS, 2, 2, 2, 2, cols, 128), BF16),
+                pltpu.VMEM((G_SLOTS,) + block + (2, cols, 128), BF16),
+                pltpu.VMEM((G_SLOTS,) + block + (cols, 128), BF16),
+                pltpu.VMEM((RS_SLOTS,) + block + (cols, 128), BF16),
+                pltpu.VMEM((IN_SLOTS, PARTS, 2, 2, cols, 128), BF16),
+                pltpu.VMEM((IN_SLOTS, PARTS, 2, cols, 128), BF16),
+                pltpu.VMEM((IN_SLOTS, PARTS, cols, 128), BF16),
+                pltpu.VMEM((AG_SLOTS,) + block + (2, cols, 128), BF16),
                 pltpu.SemaphoreType.DMA((2, 2)),
                 pltpu.SemaphoreType.DMA((2, 2)),
-                pltpu.SemaphoreType.DMA((3, PARTS, 2)),
-                pltpu.SemaphoreType.DMA((3, PARTS, 2)),
-                pltpu.SemaphoreType.DMA((3, PARTS, 2)),
-                pltpu.SemaphoreType.DMA((3, PARTS, 2)),
+                pltpu.SemaphoreType.DMA((3, PARTS, IN_SLOTS)),
+                pltpu.SemaphoreType.DMA((3, PARTS, IN_SLOTS)),
+                pltpu.SemaphoreType.DMA((3, PARTS, IN_SLOTS)),
+                pltpu.SemaphoreType.DMA((3, PARTS, IN_SLOTS)),
                 pltpu.SemaphoreType.DMA((2,)),
                 pltpu.SemaphoreType.DMA((5,)),
                 pltpu.SemaphoreType.DMA((3,)),

time: 283 us -> 272 us (0.961)
  Pallas kernels: 275 us -> 264 us
    pallas_call x1, Pallas kernels: 163 us -> 152 us  [local_step(): pl.pallas_call(functools.partial(backward_kernel, n_items), grid=(n_items...]
where the time goes in v5:
time: 272 us; the launch traced here: 271 us
  Pallas kernels  264 us (97%)
  local copies, waits for them, and re-layouts  5.19 us (2%)
    pallas_call x1, Pallas kernels, local_step(): pl.pallas_call(functools.partial(backward_kernel, n_items), grid=(n_items...  152 us
    pallas_call x1, Pallas kernels, local_step(): pl.pallas_call(functools.partial(next_kernel, n_img, n_tok, head_rows), g...  58.1 us
    pallas_call x1, Pallas kernels, local_step(): pl.pallas_call(functools.partial(forward_kernel, n_img, n_tok, n_img * n_...  54.1 us

profile of v5, /device:TPU:0, one launch (start us, length us, event | category | flops | bytes accessed | tf_op | source)
XLA Modules:
  0.0 271.3 jit_solution(12970597882232161169)
XLA Ops:
  0.6 0.0 copy-start.2
  0.6 54.1 %step_forward.1 = (bf16[32,800,192]{2,1,0:T(8,128)(2,1)}, bf16[32,800,768]{2,1,0:T(8,128)(2,1)}, bf16[800,192]{1,0:T(8,128)(2,1)}, bf16[3,2,2,2,2,48,128]{6,5,4,3,2,1,0:T(8,128)(2,1)}) custom-call(s32[4]{0:T(128)} %lab_ref.1, bf16[4,192,197]{2,1,0:T(8,128)(2,1)} %bitcast.28, f32[32,192,768]{2,1,0:T(8,128)} %wu_ref.5, f32[32,192,768]{2,1,0:T(8,128)} %bitcast.19, ...), custom_call_target="tpu_custom_call" | custom-call | tf_op jit(solution)/shard_map/step_forward/pallas_call | solution.py:458
  54.7 0.0 copy-done.2
  54.8 0.7 copy.20
  56.1 151.9 %step_backward.1 = (f32[3,48,128]{2,1,0:T(8,128)}, f32[32,48,192]{2,1,0:T(8,128)}, f32[32,48,192]{2,1,0:T(8,128)}, bf16[33,3,2,2,2,2,48,128]{7,6,5,4,3,2,1,0:T(8,128)(2,1)}) custom-call(f32[1,1]{1,0:T(1,128)} %bitcast.18.sc_ref, bf16[3,2,2,2,2,48,128]{6,5,4,3,2,1,0:T(8,128)(2,1)} %get-tuple-element.19.gh_hbm, bf16[800,192]{1,0:T(8,128)(2,1)} %get-tuple-element.20.grad_hbm, ...), custom_call_target="tpu_custom_call" | custom-call | tf_op jit(solution)/shard_map/step_backward/pallas_call | solution.py:500
  208.7 0.0 copy-start.1
  208.7 0.0 copy-start
  208.7 58.1 %step_next.1 = (f32[32,192,768]{2,1,0:T(8,128)}, f32[32,192,768]{2,1,0:T(8,128)}, f32[192,1000]{1,0:T(8,128)}, f32[4,1000]{1,0:T(4,128)}) custom-call(f32[1,1]{1,0:T(1,128)} %bitcast.17.lr_ref, bf16[4,192,197]{2,1,0:T(8,128)(2,1)} %bitcast.29, f32[32,192,768]{2,1,0:T(8,128)} %wu_ref.5, f32[32,192,768]{2,1,0:T(8,128)} %bitcast.21, ...), custom_call_target="tpu_custom_call" | custom-call | tf_op jit(solution)/shard_map/step_next/pallas_call | solution.py:552
  266.8 0.0 copy-done.1
  266.9 0.6 slice.4
  267.5 2.7 copy.29
  270.2 0.0 copy-done
  270.2 1.1 copy.30
  (4 shorter events, 0.1 us)
Async XLA Ops:
  0.6 54.1 %copy-start.2 = (f32[12,1000]{1,0:T(8,128)S(1)}, f32[12,1000]{1,0:T(8,128)}, u32[]{:S(2)}) copy-start(f32[12,1000]{1,0:T(8,128)} %param.19) | copy-start | bytes 144004
  208.7 58.2 %copy-start.1 = (f32[3,48,128]{2,1,0:T(8,128)S(1)}, f32[3,48,128]{2,1,0:T(8,128)}, u32[]{:S(2)}) copy-start(f32[3,48,128]{2,1,0:T(8,128)} %get-tuple-element.30) | copy-start | bytes 221188
  208.7 61.5 %copy-start = (f32[32,48,192]{2,1,0:T(8,128)S(1)}, f32[32,48,192]{2,1,0:T(8,128)}, u32[]{:S(2)}) copy-start(f32[32,48,192]{2,1,0:T(8,128)} %get-tuple-element.43) | copy-start | bytes 3538948

commit v6 on v5

--- a/solution.py
+++ b/solution.py
@@ -44,6 +44,11 @@
 def gelu(values):
     inner = values * (GELU_C + (GELU_C * GELU_A) * (values * values))
     return values * (0.5 + 0.5 * jnp.tanh(inner))
+
+
+def gelu_half(half):
+    tanh_v = jnp.tanh(half * (2.0 * GELU_C + (8.0 * GELU_C * GELU_A) * (half * half)))
+    return half + half * tanh_v
 
 
 def gelu_both(values):
@@ -147,12 +152,16 @@
 
 
 def next_kernel(
-    n_img, n_tok, head_rows, lr_ref, x_hbm, wu_ref, wd_ref, mom_ref, all_hbm, wh_hbm, nwu_ref, nwd_ref, nwh_hbm, log_hbm,
-    x_ref, wh_ref, mh_ref, log_ref, wide, rows, sems,
+    n_img, n_tok, head_rows, lr_ref, x_hbm, wu_ref, wd_ref, mom_ref, all_hbm, wh_hbm, mh_in, mu_in, md_in,
+    nwu_ref, nwd_ref, nwh_hbm, log_hbm, mh_out, mu_out, md_out,
+    x_ref, wh_ref, mh_ref, log_ref, wide, rows, keep_h, keep_u, keep_d, sems,
 ):
     layer = pl.program_id(0)
     x_copy = pltpu.make_async_copy(x_hbm, x_ref, sems.at[0])
     wh_copy = pltpu.make_async_copy(wh_hbm, wh_ref, sems.at[1])
+    kept = ((mh_in, keep_h, mh_out), (mu_in, keep_u, mu_out), (md_in, keep_d, md_out))
+    takes = tuple(pltpu.make_async_copy(src, ref, sems.at[3 + i]) for i, (src, ref, _) in enumerate(kept))
+    gives = tuple(pltpu.make_async_copy(ref, dst, sems.at[3 + i]) for i, (_, ref, dst) in enumerate(kept))
     mh_copy = pltpu.make_async_copy(all_hbm.at[all_hbm.shape[0] - 1], mh_ref, sems.at[2])
 
     @pl.when(layer == 0)
@@ -160,8 +169,17 @@
         x_copy.start()
         wh_copy.start()
         mh_copy.start()
+        for copy in takes:
+            copy.start()
         x_copy.wait()
         pack_rows(x_ref, wide, rows, n_img, n_tok)
+
+    @pl.when(layer == pl.num_programs(0) // 2)
+    def _():
+        for copy in takes:
+            copy.wait()
+        for copy in gives:
+            copy.start()
 
     rate = lr_ref[0, 0]
     step = rows.shape[0] // CHUNKS
@@ -171,15 +189,15 @@
         nwu_ref[sub, 128:, :] = wu_ref[sub, 128:, :] - rate * mixed[64:, :]
         nwd_ref[sub, :128, :] = wd_ref[sub, :128, :] - rate * mom_ref[sub, 1].T.astype(F32)
         nwd_ref[sub, 128:, :] = wd_ref[sub, 128:, :] - rate * mixed[:64, :]
-        up_b = nwu_ref[sub].astype(BF16)
+        up_b = nwu_ref[sub].astype(BF16) * 0.5
         down_b = nwd_ref[sub].astype(BF16)
         for chunk in range(CHUNKS):
             sl = slice(chunk * step, (chunk + 1) * step)
             x_wide = rows[sl, :].astype(F32)
             centered, scale = norm_parts(x_wide)
             u_rows = (centered * scale).astype(BF16)
-            pre = jnp.dot(u_rows, up_b, preferred_element_type=F32).astype(BF16)
-            z_rows = gelu(pre.astype(F32)).astype(BF16)
+            half = jnp.dot(u_rows, up_b, preferred_element_type=F32).astype(BF16)
+            z_rows = gelu_half(half.astype(F32)).astype(BF16)
             y_rows = lax.dot_general(z_rows, down_b, LAST, preferred_element_type=F32).astype(BF16)
             rows[sl, :] = (x_wide + y_rows.astype(F32)).astype(BF16)
 
@@ -203,11 +221,13 @@
         log_copy.start()
         log_copy.wait()
         out_copy.wait()
+        for copy in gives:
+            copy.wait()
 
 
 def backward_kernel(
     n_items, sc_ref, gh_hbm, grad_hbm, xs_ref, pre_ref, wu_ref, wd_ref, mh_hbm, mu_hbm, md_hbm, nmh_hbm, nmu_hbm, nmd_hbm, all_ref,
-    g_rows, z_buf, da_buf, u_buf, mh_ref, mu_ref, md_ref, g_buf, pair_buf, sum_buf, rcv0, rcv1, rcv2, ag_buf,
+    g_rows, z_buf, da_buf, u_buf, mh_wide, mh_ref, mu_ref, md_ref, g_buf, pair_buf, sum_buf, rcv0, rcv1, rcv2, ag_buf,
     d2d_send, d2d_recv, rs_send, rs_recv, ag_send, ag_recv, out_sem, in_sem, mom_sem,
 ):
     t = pl.program_id(0)
@@ -350,10 +370,16 @@
         def _():
             for copy in moms:
                 copy.wait()
+            head_rows, n_cls = mh_ref.shape
+            mh_wide[...] = jnp.zeros_like(mh_wide)
+            mh_wide[:head_rows, :n_cls] = mh_ref[...]
             for part in range(PARTS):
-                mom = sc_ref[0, 0] * mh_ref[part] + reduced(part)
-                mh_ref[part] = mom
+                lanes = [slice((3 * part + i) * 128, (3 * part + i + 1) * 128) for i in range(3)]
+                mom = sc_ref[0, 0] * jnp.concatenate([mh_wide[:, one] for one in lanes], axis=0) + reduced(part)
+                for i in range(3):
+                    mh_wide[:, lanes[i]] = mom[i * 16 : (i + 1) * 16, :]
                 hand_on(part, mom)
+            mh_ref[...] = mh_wide[:head_rows, :n_cls]
 
         @pl.when(t > UPDATE)
         def _():
@@ -490,14 +516,11 @@
             name="step_forward",
         )(labels, x_now.transpose(0, 2, 1), w_up, down_t, w_head)
 
-        head_m = jnp.pad(mom_head, ((0, 16 - head_rows), (0, 9 * 128 - n_cls))).reshape(16, 9, 128)
-        head_m = head_m.transpose(1, 0, 2).reshape(PARTS, cols, 128)
-
         def layer_at(t):
             return jnp.clip(n_items - 1 - t, 0, n_layers - 1)
 
         block = (PARTS, 2, 2, 2)
-        mom_head_new, mom_up_new, new_mom_down, gathered = pl.pallas_call(
+        head_kept, up_kept, down_kept, gathered = pl.pallas_call(
             functools.partial(backward_kernel, n_items),
             grid=(n_items + TWIN + 2,),
             in_specs=[
@@ -514,7 +537,7 @@
             ],
             out_specs=[any_spec] * 4,
             out_shape=[
-                jax.ShapeDtypeStruct((PARTS, cols, 128), F32),
+                jax.ShapeDtypeStruct(mom_head.shape, F32),
                 jax.ShapeDtypeStruct((n_layers, cols, width), F32),
                 jax.ShapeDtypeStruct((n_layers, cols, width), F32),
                 jax.ShapeDtypeStruct((n_items, PARTS, 2, 2, 2, 2, cols, 128), BF16),
@@ -524,7 +547,8 @@
                 pltpu.VMEM((n_rows, hidden), BF16),
                 pltpu.VMEM((n_rows, hidden), BF16),
                 pltpu.VMEM((n_rows, width), BF16),
-                pltpu.VMEM((PARTS, cols, 128), F32),
+                pltpu.VMEM((16, 9 * 128), F32),
+                pltpu.VMEM(mom_head.shape, F32),
                 pltpu.VMEM((n_layers, cols, width), F32),
                 pltpu.VMEM((n_layers, cols, width), F32),
                 pltpu.VMEM((G_SLOTS,) + block + (2, cols, 128), BF16),
@@ -546,10 +570,10 @@
             ],
             compiler_params=pltpu.CompilerParams(vmem_limit_bytes=VMEM_LIMIT, collective_id=0, has_side_effects=True),
             name="step_backward",
-        )(mom_decay.reshape(1, 1), head_g, grad_rows, xs, pre, w_up, down_t, head_m, mom_up.transpose(0, 2, 1), mom_down)
+        )(mom_decay.reshape(1, 1), head_g, grad_rows, xs, pre, w_up, down_t, mom_head, mom_up.transpose(0, 2, 1), mom_down)
 
         gathered = gathered.reshape(n_items, PARTS, n_dev * cols, 128)
-        new_w_up, new_down_t, new_w_head, logits = pl.pallas_call(
+        new_w_up, new_down_t, new_w_head, logits, new_mom_head, mom_up_new, new_mom_down = pl.pallas_call(
             functools.partial(next_kernel, n_img, n_tok, head_rows),
             grid=(n_layers // per,),
             in_specs=[
@@ -560,18 +584,23 @@
                 pl.BlockSpec((per, PARTS, n_dev * cols, 128), lambda i: (i, 0, 0, 0)),
                 any_spec,
                 any_spec,
+                any_spec,
+                any_spec,
+                any_spec,
             ],
             out_specs=[
                 pl.BlockSpec((per, width, hidden), lambda i: (i, 0, 0)),
                 pl.BlockSpec((per, width, hidden), lambda i: (i, 0, 0)),
-                any_spec,
-                any_spec,
-            ],
+            ]
+            + [any_spec] * 5,
             out_shape=[
                 jax.ShapeDtypeStruct(w_up.shape, F32),
                 jax.ShapeDtypeStruct(w_up.shape, F32),
                 jax.ShapeDtypeStruct(w_head.shape, F32),
                 jax.ShapeDtypeStruct((n_img, n_cls), F32),
+                jax.ShapeDtypeStruct(mom_head.shape, F32),
+                jax.ShapeDtypeStruct((n_layers, cols, width), F32),
+                jax.ShapeDtypeStruct((n_layers, cols, width), F32),
             ],
             scratch_shapes=[
                 pltpu.VMEM((n_img, width, n_tok), BF16),
@@ -580,13 +609,15 @@
                 pltpu.VMEM((n_img, n_cls), F32),
                 pltpu.VMEM((n_rows, width), F32),
                 pltpu.VMEM((n_rows, width), BF16),
-                pltpu.SemaphoreType.DMA((3,)),
+                pltpu.VMEM(mom_head.shape, F32),
+                pltpu.VMEM((n_layers, cols, width), F32),
+                pltpu.VMEM((n_layers, cols, width), F32),
+                pltpu.SemaphoreType.DMA((6,)),
             ],
             compiler_params=pltpu.CompilerParams(vmem_limit_bytes=VMEM_LIMIT),
             name="step_next",
-        )(learn_rate.reshape(1, 1), x_next.transpose(0, 2, 1), w_up, down_t, gathered, gathered, w_head)
-
-        new_mom_head = mom_head_new.reshape(9, 16, 128).transpose(1, 0, 2).reshape(16, 9 * 128)[:head_rows, :n_cls]
+        )(learn_rate.reshape(1, 1), x_next.transpose(0, 2, 1), w_up, down_t, gathered, gathered, w_head, head_kept, up_kept, down_kept)
+
         return (logits, new_w_up, new_down_t.transpose(0, 2, 1), new_w_head, mom_up_new.transpose(0, 2, 1), new_mom_down, new_mom_head)
 
     spec_up = P(None, None, "data")

time: 272 us -> 264 us (0.971)
  local copies, waits for them, and re-layouts: 5.19 us -> 0 us
    unnamed x9 -> x0, local copies, waits for them, and re-layouts: 3.84 us -> none
where the time goes in v6:
time: 264 us
  Pallas kernels  262 us (99%)
    pallas_call x1, Pallas kernels, local_step(): pl.pallas_call(functools.partial(backward_kernel, n_items), grid=(n_items...  152 us
    pallas_call x1, Pallas kernels, local_step(): pl.pallas_call(functools.partial(next_kernel, n_img, n_tok, head_rows), g...  56.2 us
    pallas_call x1, Pallas kernels, local_step(): pl.pallas_call(functools.partial(forward_kernel, n_img, n_tok, n_img * n_...  54.1 us

profile of v6, /device:TPU:0, one launch (start us, length us, event | category | flops | bytes accessed | tf_op | source)
XLA Modules:
  0.0 264.2 jit_solution(17316226025237381505)
XLA Ops:
  0.6 54.1 %step_forward.1 = (bf16[32,800,192]{2,1,0:T(8,128)(2,1)}, bf16[32,800,768]{2,1,0:T(8,128)(2,1)}, bf16[800,192]{1,0:T(8,128)(2,1)}, bf16[3,2,2,2,2,48,128]{6,5,4,3,2,1,0:T(8,128)(2,1)}) custom-call(s32[4]{0:T(128)} %lab_ref.1, bf16[4,192,197]{2,1,0:T(8,128)(2,1)} %bitcast.17, f32[32,192,768]{2,1,0:T(8,128)} %wu_ref.5, f32[32,192,768]{2,1,0:T(8,128)} %bitcast.11, ...), custom_call_target="tpu_custom_call" | custom-call | tf_op jit(solution)/shard_map/step_forward/pallas_call | solution.py:484
  55.3 152.0 %step_backward.1 = (f32[12,1000]{1,0:T(8,128)}, f32[32,48,192]{2,1,0:T(8,128)}, f32[32,48,192]{2,1,0:T(8,128)}, bf16[33,3,2,2,2,2,48,128]{7,6,5,4,3,2,1,0:T(8,128)(2,1)}) custom-call(f32[1,1]{1,0:T(1,128)} %bitcast.10.sc_ref, bf16[3,2,2,2,2,48,128]{6,5,4,3,2,1,0:T(8,128)(2,1)} %get-tuple-element.22.gh_hbm, bf16[800,192]{1,0:T(8,128)(2,1)} %get-tuple-element.23.grad_hbm, ...), custom_call_target="tpu_custom_call" | custom-call | tf_op jit(solution)/shard_map/step_backward/pallas_call | solution.py:523
  208.0 56.2 %step_next.1 = (f32[32,192,768]{2,1,0:T(8,128)}, f32[32,192,768]{2,1,0:T(8,128)}, f32[192,1000]{1,0:T(8,128)}, f32[4,1000]{1,0:T(4,128)}, f32[12,1000]{1,0:T(8,1...) custom-call(f32[1,1]{1,0:T(1,128)} %bitcast.9.lr_ref, bf16[4,192,197]{2,1,0:T(8,128)(2,1)} %bitcast.18, ...), custom_call_target="tpu_custom_call" | custom-call | tf_op jit(solution)/shard_map/step_next/pallas_call | solution.py:576

commit v7 on v6

--- a/solution.py
+++ b/solution.py
@@ -16,13 +16,13 @@
 ROWS = (((0,), (0,)), ((), ()))
 MESH_ID = pl.DeviceIdType.MESH
 VMEM_LIMIT = 62 * 1024 * 1024
-CHUNKS = 5
+CHUNKS = 1
 G_SLOTS = 2
-RS_SLOTS = 8
+RS_SLOTS = 4
 IN_SLOTS = 4
 AG_SLOTS = 12
-UPDATE = 7
-TWIN = 13
+UPDATE = 4
+TWIN = 10
 PARTS = 3
 POOL = 16
 ORDER = ((0, 1, 2), (1, 2, 0), (2, 0, 1))
@@ -399,9 +399,9 @@
 
     for stage in (1, 0):
 
-        @pl.when(at_lag(3 + 2 * stage))
+        @pl.when(at_lag(2 + stage))
         def _(stage=stage):
-            item = t - 3 - 2 * stage
+            item = t - 2 - stage
             for part in range(PARTS):
                 rs_copy(item, stage, part).wait()
                 kept = (lax.rem(item, RS_SLOTS), part) + cut(part, stage, place[ORDER[part][stage]])

time: 264 us -> 261 us (0.989)
  Pallas kernels: 262 us -> 259 us
    pallas_call x1, Pallas kernels: 56.2 us -> 52.8 us  [local_step(): pl.pallas_call(functools.partial(next_kernel, n_img, n_tok, head_rows), g...]
where the time goes in v7:
time: 261 us
  Pallas kernels  259 us (99%)
    pallas_call x1, Pallas kernels, local_step(): pl.pallas_call(functools.partial(backward_kernel, n_items), grid=(n_items...  154 us
    pallas_call x1, Pallas kernels, local_step(): pl.pallas_call(functools.partial(next_kernel, n_img, n_tok, head_rows), g...  52.8 us
    pallas_call x1, Pallas kernels, local_step(): pl.pallas_call(functools.partial(forward_kernel, n_img, n_tok, n_img * n_...  52.6 us

profile of v7, /device:TPU:0, one launch (start us, length us, event | category | flops | bytes accessed | tf_op | source)
XLA Modules:
  0.0 260.8 jit_solution(13918504273826355796)
XLA Ops:
  0.6 52.6 %step_forward.1 = (bf16[32,800,192]{2,1,0:T(8,128)(2,1)}, bf16[32,800,768]{2,1,0:T(8,128)(2,1)}, bf16[800,192]{1,0:T(8,128)(2,1)}, bf16[3,2,2,2,2,48,128]{6,5,4,3,2,1,0:T(8,128)(2,1)}) custom-call(s32[4]{0:T(128)} %lab_ref.1, bf16[4,192,197]{2,1,0:T(8,128)(2,1)} %bitcast.17, f32[32,192,768]{2,1,0:T(8,128)} %wu_ref.5, f32[32,192,768]{2,1,0:T(8,128)} %bitcast.11, ...), custom_call_target="tpu_custom_call" | custom-call | tf_op jit(solution)/shard_map/step_forward/pallas_call | solution.py:484
  53.9 153.5 %step_backward.1 = (f32[12,1000]{1,0:T(8,128)}, f32[32,48,192]{2,1,0:T(8,128)}, f32[32,48,192]{2,1,0:T(8,128)}, bf16[33,3,2,2,2,2,48,128]{7,6,5,4,3,2,1,0:T(8,128)(2,1)}) custom-call(f32[1,1]{1,0:T(1,128)} %bitcast.10.sc_ref, bf16[3,2,2,2,2,48,128]{6,5,4,3,2,1,0:T(8,128)(2,1)} %get-tuple-element.22.gh_hbm, bf16[800,192]{1,0:T(8,128)(2,1)} %get-tuple-element.23.grad_hbm, ...), custom_call_target="tpu_custom_call" | custom-call | tf_op jit(solution)/shard_map/step_backward/pallas_call | solution.py:523
  208.0 52.8 %step_next.1 = (f32[32,192,768]{2,1,0:T(8,128)}, f32[32,192,768]{2,1,0:T(8,128)}, f32[192,1000]{1,0:T(8,128)}, f32[4,1000]{1,0:T(4,128)}, f32[12,1000]{1,0:T(8,1...) custom-call(f32[1,1]{1,0:T(1,128)} %bitcast.9.lr_ref, bf16[4,192,197]{2,1,0:T(8,128)(2,1)} %bitcast.18, ...), custom_call_target="tpu_custom_call" | custom-call | tf_op jit(solution)/shard_map/step_next/pallas_call | solution.py:576

commit v8 on v6

--- a/solution.py
+++ b/solution.py
@@ -16,7 +16,7 @@
 ROWS = (((0,), (0,)), ((), ()))
 MESH_ID = pl.DeviceIdType.MESH
 VMEM_LIMIT = 62 * 1024 * 1024
-CHUNKS = 5
+CHUNKS = 1
 G_SLOTS = 2
 RS_SLOTS = 8
 IN_SLOTS = 4

time: 264 us -> 259 us (0.981)
  Pallas kernels: 262 us -> 256 us
    pallas_call x1, Pallas kernels: 56.2 us -> 52.8 us  [local_step(): pl.pallas_call(functools.partial(next_kernel, n_img, n_tok, head_rows), g...]
where the time goes in v8:
time: 259 us; the launch traced here: 258 us
  Pallas kernels  256 us (99%)
    pallas_call x1, Pallas kernels, local_step(): pl.pallas_call(functools.partial(backward_kernel, n_items), grid=(n_items...  151 us
    pallas_call x1, Pallas kernels, local_step(): pl.pallas_call(functools.partial(next_kernel, n_img, n_tok, head_rows), g...  52.8 us
    pallas_call x1, Pallas kernels, local_step(): pl.pallas_call(functools.partial(forward_kernel, n_img, n_tok, n_img * n_...  52.6 us

profile of v8, /device:TPU:0, one launch (start us, length us, event | category | flops | bytes accessed | tf_op | source)
XLA Modules:
  0.0 258.3 jit_solution(18270474941548186725)
XLA Ops:
  0.6 52.6 %step_forward.1 = (bf16[32,800,192]{2,1,0:T(8,128)(2,1)}, bf16[32,800,768]{2,1,0:T(8,128)(2,1)}, bf16[800,192]{1,0:T(8,128)(2,1)}, bf16[3,2,2,2,2,48,128]{6,5,4,3,2,1,0:T(8,128)(2,1)}) custom-call(s32[4]{0:T(128)} %lab_ref.1, bf16[4,192,197]{2,1,0:T(8,128)(2,1)} %bitcast.17, f32[32,192,768]{2,1,0:T(8,128)} %wu_ref.5, f32[32,192,768]{2,1,0:T(8,128)} %bitcast.11, ...), custom_call_target="tpu_custom_call" | custom-call | tf_op jit(solution)/shard_map/step_forward/pallas_call | solution.py:484
  53.9 151.0 %step_backward.1 = (f32[12,1000]{1,0:T(8,128)}, f32[32,48,192]{2,1,0:T(8,128)}, f32[32,48,192]{2,1,0:T(8,128)}, bf16[33,3,2,2,2,2,48,128]{7,6,5,4,3,2,1,0:T(8,128)(2,1)}) custom-call(f32[1,1]{1,0:T(1,128)} %bitcast.10.sc_ref, bf16[3,2,2,2,2,48,128]{6,5,4,3,2,1,0:T(8,128)(2,1)} %get-tuple-element.22.gh_hbm, bf16[800,192]{1,0:T(8,128)(2,1)} %get-tuple-element.23.grad_hbm, ...), custom_call_target="tpu_custom_call" | custom-call | tf_op jit(solution)/shard_map/step_backward/pallas_call | solution.py:523
  205.5 52.8 %step_next.1 = (f32[32,192,768]{2,1,0:T(8,128)}, f32[32,192,768]{2,1,0:T(8,128)}, f32[192,1000]{1,0:T(8,128)}, f32[4,1000]{1,0:T(4,128)}, f32[12,1000]{1,0:T(8,1...) custom-call(f32[1,1]{1,0:T(1,128)} %bitcast.9.lr_ref, bf16[4,192,197]{2,1,0:T(8,128)(2,1)} %bitcast.18, ...), custom_call_target="tpu_custom_call" | custom-call | tf_op jit(solution)/shard_map/step_next/pallas_call | solution.py:576
